TPU v7x, 16 devices: a whole 2x2x2 slice. The times are simulated.
16 devices in a mesh: sp: 16 (over z, y, x, core).
Axes of the slice: x: 2, y: 2, z: 2, core: 2. Of those that a mesh axis runs over, the one named last changes fastest.
Arguments:
- hidden: bfloat16 [32, 512, 1024], P(None, 'sp')
- norm_gain: float32 [1024], replicated
- w_q: bfloat16 [1024, 2048], replicated
- w_k: bfloat16 [1024, 1024], replicated
- w_v: bfloat16 [1024, 1024], replicated
- q_gain: float32 [128], replicated
- k_gain: float32 [128], replicated
- w_o: bfloat16 [2048, 1024], replicated
- d_out: bfloat16 [32, 512, 1024], P(None, 'sp')
Outputs:
- output 1: bfloat16 [32, 512, 1024], P(None, 'sp')
- output 2: bfloat16 [32, 512, 1024], P(None, 'sp')
- output 3: float32 [1024, 2048], replicated
- output 4: float32 [1024, 1024], replicated
- output 5: float32 [1024, 1024], replicated
- output 6: float32 [2048, 1024], replicated
- output 7: float32 [1024], replicated
- output 8: float32 [128], replicated
- output 9: float32 [128], replicated
All inputs are finite; a program needn't handle non-finite values.
Results may differ from a plain program's by a relative error of at most 0.0181044.
Values are sent between devices in bfloat16 or wider.
A program may use at most 1 GiB of HBM per device.

v0:
```python
import math
import jax
import jax.numpy as jnp
from jax import lax
from jax.sharding import PartitionSpec as P

ROPE_BASE = 1000000.0
NORM_EPS = 1e-6


def rms_scale(values, gain):
    return values * lax.rsqrt(jnp.mean(values * values, axis=-1, keepdims=True) + NORM_EPS) * gain


def rope_tables(positions, head_dim):
    half_dim = head_dim // 2
    inv_freq = jnp.exp(jnp.arange(half_dim).astype(jnp.float32) * (-2.0 * math.log(ROPE_BASE) / head_dim))
    angles = positions[:, None] * inv_freq[None, :]
    return jnp.cos(angles), jnp.sin(angles)


def qk_post(raw, gain, cos_tab, sin_tab):
    normed = rms_scale(raw, gain)
    half_dim = raw.shape[-1] // 2
    first = normed[..., :half_dim]
    second = normed[..., half_dim:]
    cos_b = cos_tab[None, :, None, :]
    sin_b = sin_tab[None, :, None, :]
    return jnp.concatenate([first * cos_b - second * sin_b, second * cos_b + first * sin_b], axis=-1)


def core_forward(q_part, k_part, v_part):
    n_batch, n_pos, q_heads, head_dim = q_part.shape
    kv_heads = k_part.shape[2]
    q_grouped = q_part.reshape(n_batch, n_pos, kv_heads, q_heads // kv_heads, head_dim)
    scores = jnp.einsum('bqkgd,bskd->bkgqs', q_grouped, k_part, preferred_element_type=jnp.float32) * head_dim ** -0.5
    causal = lax.broadcasted_iota(jnp.int32, (n_pos, n_pos), 0) >= lax.broadcasted_iota(jnp.int32, (n_pos, n_pos), 1)
    scores = jnp.where(causal, scores, -1e30)
    attn_prob = jax.nn.softmax(scores, axis=-1)
    prob_bf = attn_prob.astype(jnp.bfloat16)
    out_heads = jnp.einsum('bkgqs,bskd->bqkgd', prob_bf, v_part, preferred_element_type=jnp.float32)
    return out_heads.astype(jnp.bfloat16).reshape(n_batch, n_pos, q_heads, head_dim), attn_prob, prob_bf


def core_backward(q_part, k_part, v_part, attn_prob, prob_bf, d_heads):
    n_batch, n_pos, q_heads, head_dim = q_part.shape
    kv_heads = k_part.shape[2]
    grouped_shape = (n_batch, n_pos, kv_heads, q_heads // kv_heads, head_dim)
    q_grouped = q_part.reshape(grouped_shape)
    d_grouped = d_heads.reshape(grouped_shape)
    d_prob = jnp.einsum('bqkgd,bskd->bkgqs', d_grouped, v_part, preferred_element_type=jnp.float32)
    d_scores = attn_prob * (d_prob - jnp.sum(attn_prob * d_prob, axis=-1, keepdims=True))
    d_scores = (d_scores * head_dim ** -0.5).astype(jnp.bfloat16)
    d_q = jnp.einsum('bkgqs,bskd->bqkgd', d_scores, k_part, preferred_element_type=jnp.float32)
    d_k = jnp.einsum('bkgqs,bqkgd->bskd', d_scores, q_grouped, preferred_element_type=jnp.float32)
    d_v = jnp.einsum('bkgqs,bqkgd->bskd', prob_bf, d_grouped, preferred_element_type=jnp.float32)
    return d_q.astype(jnp.bfloat16).reshape(n_batch, n_pos, q_heads, head_dim), d_k, d_v


def solution(mesh):
    n_dev = mesh.shape['sp']
    seq_spec = P(None, 'sp', None)
    replicated = P()

    def local_step(hidden, norm_gain, w_q, w_k, w_v, q_gain, k_gain, w_o, d_out):
        n_batch, seq_loc = hidden.shape[0], hidden.shape[1]
        head_dim = q_gain.shape[0]
        q_heads = w_q.shape[1] // head_dim
        kv_heads = w_k.shape[1] // head_dim
        copies = max(n_dev // kv_heads, 1)
        q_shape = (n_batch, seq_loc, q_heads, head_dim)
        kv_shape = (n_batch, seq_loc, kv_heads, head_dim)
        row_start = lax.axis_index('sp') * seq_loc
        positions = (row_start + jnp.arange(seq_loc)).astype(jnp.float32)
        cos_tab, sin_tab = rope_tables(positions, head_dim)
        hidden_f = hidden.astype(jnp.float32)
        normed_f, norm_back = jax.vjp(rms_scale, hidden_f, norm_gain)
        normed = normed_f.astype(jnp.bfloat16)
        q_raw = jnp.einsum('bsd,de->bse', normed, w_q, preferred_element_type=jnp.float32).astype(jnp.bfloat16)
        k_raw = jnp.einsum('bsd,de->bse', normed, w_k, preferred_element_type=jnp.float32).astype(jnp.bfloat16)
        v_raw = jnp.einsum('bsd,de->bse', normed, w_v, preferred_element_type=jnp.float32).astype(jnp.bfloat16)

        def post_both(q_in, k_in, q_scale, k_scale):
            return qk_post(q_in, q_scale, cos_tab, sin_tab), qk_post(k_in, k_scale, cos_tab, sin_tab)

        (q_rot, k_rot), post_back = jax.vjp(post_both, q_raw.astype(jnp.float32).reshape(q_shape), k_raw.astype(jnp.float32).reshape(kv_shape), q_gain, k_gain)
        k_rep = jnp.repeat(k_rot.astype(jnp.bfloat16), copies, axis=2)
        v_rep = jnp.repeat(v_raw.reshape(kv_shape), copies, axis=2)
        q_here = lax.all_to_all(q_rot.astype(jnp.bfloat16), 'sp', 2, 1, tiled=True)
        k_here = lax.all_to_all(k_rep, 'sp', 2, 1, tiled=True)
        v_here = lax.all_to_all(v_rep, 'sp', 2, 1, tiled=True)
        o_here, attn_prob, prob_bf = core_forward(q_here, k_here, v_here)
        attn = lax.all_to_all(o_here, 'sp', 1, 2, tiled=True).reshape(n_batch, seq_loc, q_heads * head_dim)
        y_out = (hidden_f + jnp.einsum('bse,ed->bsd', attn, w_o, preferred_element_type=jnp.float32)).astype(jnp.bfloat16)
        d_attn = jnp.einsum('bsd,ed->bse', d_out, w_o, preferred_element_type=jnp.float32).astype(jnp.bfloat16)
        d_wo = jnp.einsum('bse,bsd->ed', attn, d_out, preferred_element_type=jnp.float32)
        d_o_here = lax.all_to_all(d_attn.reshape(q_shape), 'sp', 2, 1, tiled=True)
        dq_here, dk_here, dv_here = core_backward(q_here, k_here, v_here, attn_prob, prob_bf, d_o_here)
        dq_loc = lax.all_to_all(dq_here, 'sp', 1, 2, tiled=True)
        dk_parts = lax.all_to_all(dk_here.astype(jnp.bfloat16), 'sp', 1, 2, tiled=True)
        dv_parts = lax.all_to_all(dv_here.astype(jnp.bfloat16), 'sp', 1, 2, tiled=True)
        split_shape = (n_batch, seq_loc, kv_heads, copies, head_dim)
        dk_sum = jnp.sum(dk_parts.reshape(split_shape).astype(jnp.float32), axis=3).astype(jnp.bfloat16)
        dv_sum = jnp.sum(dv_parts.reshape(split_shape).astype(jnp.float32), axis=3).astype(jnp.bfloat16)
        dq_raw_f, dk_raw_f, d_qgain, d_kgain = post_back((dq_loc.astype(jnp.float32), dk_sum.astype(jnp.float32)))
        dq_raw = dq_raw_f.astype(jnp.bfloat16).reshape(n_batch, seq_loc, q_heads * head_dim)
        dk_raw = dk_raw_f.astype(jnp.bfloat16).reshape(n_batch, seq_loc, kv_heads * head_dim)
        dv_raw = dv_sum.reshape(n_batch, seq_loc, kv_heads * head_dim)
        d_wq = jnp.einsum('bsd,bse->de', normed, dq_raw, preferred_element_type=jnp.float32)
        d_wk = jnp.einsum('bsd,bse->de', normed, dk_raw, preferred_element_type=jnp.float32)
        d_wv = jnp.einsum('bsd,bse->de', normed, dv_raw, preferred_element_type=jnp.float32)
        d_normed = (jnp.einsum('bse,de->bsd', dq_raw, w_q, preferred_element_type=jnp.float32) + jnp.einsum('bse,de->bsd', dk_raw, w_k, preferred_element_type=jnp.float32) + jnp.einsum('bse,de->bsd', dv_raw, w_v, preferred_element_type=jnp.float32))
        dx_f, d_ngain = norm_back(d_normed)
        d_hidden = (d_out.astype(jnp.float32) + dx_f).astype(jnp.bfloat16)
        return (y_out, d_hidden, lax.psum(d_wq, 'sp'), lax.psum(d_wk, 'sp'), lax.psum(d_wv, 'sp'), lax.psum(d_wo, 'sp'), lax.psum(d_ngain, 'sp'), lax.psum(d_qgain, 'sp'), lax.psum(d_kgain, 'sp'))

    return jax.shard_map(local_step, mesh=mesh, in_specs=(seq_spec, replicated, replicated, replicated, replicated, replicated, replicated, replicated, seq_spec), out_specs=(seq_spec, seq_spec, replicated, replicated, replicated, replicated, replicated, replicated, replicated), check_vma=False)
```

profile of v0, /device:TPU:0, one launch (start us, length us, event | category | flops | bytes accessed | tf_op | source)
XLA Modules:
  0.0 893.6 jit_solution(8910127065551991953)
XLA Ops:
  10.0 7.0 convert_convert_fusion
  23.1 5.3 fusion.16
  37.2 5.7 all-to-all-start.2
  42.8 4.0 convert_convert_fusion.1
  59.0 37.3 %all-to-all-done.2 = bf16[32,32,16,128]{3,1,0,2:T(8,128)(2,1)} async-done(((bf16[32,32,16,128]{3,1,0,2:T(8,128)(2,1)}), bf16[32,32,16,128]{3,1,0,2:T(8,128)(2,1)}, u32[]{:S(2)}, u32[]{:S(2)}) %all-to-all-start.2) | async-done | bytes 4194336 | tf_op jit(solution)/shard_map/all_to_all | solution.py:89
  96.3 4.5 broadcast_in_dim.20
  100.8 5.0 all-to-all-start.1
  105.7 7.4 convert_bitcast_fusion.4
  116.1 43.1 %all-to-all-done.1 = bf16[32,32,16,128]{3,1,0,2:T(8,128)(2,1)} async-done(((bf16[32,32,16,128]{3,1,0,2:T(8,128)(2,1)}), bf16[32,32,16,128]{3,1,0,2:T(8,128)(2,1)}, u32[]{:S(2)}, u32[]{:S(2)}) %all-to-all-start.1) | async-done | bytes 4194336 | tf_op jit(solution)/shard_map/all_to_all | solution.py:90
  159.2 4.4 all-to-all-start.4
  163.7 4.6 convert_bitcast_fusion.6
  170.1 5.4 copy.229
  175.5 5.5 copy.225
  181.0 36.2 %all-to-all-done.4 = bf16[32,32,16,128]{3,1,0,2:T(8,128)(2,1)} async-done(((bf16[32,32,16,128]{3,1,0,2:T(8,128)(2,1)}), bf16[32,32,16,128]{3,1,0,2:T(8,128)(2,1)}, u32[]{:S(2)}, u32[]{:S(2)}) %all-to-all-start.4) | async-done | bytes 4194336 | tf_op jit(solution)/shard_map/all_to_all | solution.py:97
  217.1 4.5 broadcast_in_dim.18
  221.6 4.6 all-to-all-start
  226.2 5.4 copy.236
  231.7 16.6 %fusion.6 = (f32[32,512]{1,0:T(8,128)S(1)}, f32[32,512,512]{2,1,0:T(8,128)}) fusion(pred[512,512]{0,1:T(8,128)(4,1)S(1)} %iota_compare_fusion, bf16[32,512,128]{2,1,0:T(8,128)(2,1)} %bitcast.271, bf16[32,512,128]{2,1,0:T(8,128)(2,1)} %bitcast.269), kind=kOutput, calls=%fused_computation.10 | convolution fusion | flops 2172633088 | bytes 42270720 | tf_op jit(solution)/shard_map/bqkgd,bskd->bkgqs/dot_general | solution.py:36
  248.3 14.6 %fusion.5 = f32[32,512]{1,0:T(8,128)S(1)} fusion(f32[32,512,512]{2,1,0:T(8,128)} %get-tuple-element.33, f32[32,512]{1,0:T(8,128)S(1)} %get-tuple-element.32, pred[512,512]{0,1:T(8,128)(4,1)S(1)} %iota_compare_fusion), kind=kLoop, calls=%fused_computation.9 | loop fusion | flops 33538048 | bytes 33947648 | tf_op jit(solution)/shard_map/reduce_sum | solution.py:39
  262.9 16.8 %all-to-all-done = bf16[32,32,16,128]{3,1,0,2:T(8,128)(2,1)} async-done(((bf16[32,32,16,128]{3,1,0,2:T(8,128)(2,1)}), bf16[32,32,16,128]{3,1,0,2:T(8,128)(2,1)}, u32[]{:S(2)}, u32[]{:S(2)}) %all-to-all-start) | async-done | bytes 4194336 | tf_op jit(solution)/shard_map/all_to_all | solution.py:91
  283.2 26.8 %fusion = (f32[32,512]{1,0:T(8,128)S(1)}, f32[32,512,512]{2,1,0:T(8,128)}) fusion(f32[32,512]{1,0:T(8,128)S(1)} %fusion.5, f32[32,512]{1,0:T(8,128)S(1)} %get-tuple-element.32, f32[32,512,512]{2,1,0:T(8,128)} %get-tuple-element.33, pred[512,512]{0,1:T(8,128)(4,1)S(1)} %iota_compare_fusion, bf16[32,512,128]{2,1,0:T(8,128)(2,1)S(1)} %bitcast.290, ...), kind=kOutput, calls=%fused_computation.3 | convolution fusion | flops 2197798912 | bytes 75956224 | tf_op jit(solution)/shard_map/bqkgd,bskd->bkgqs/dot_general | solution.py:51
  310.0 28.2 %fusion.7 = bf16[32,512,512]{1,2,0:T(8,128)(2,1)} fusion(f32[32,512,512]{2,1,0:T(8,128)} %get-tuple-element.35, f32[32,512]{1,0:T(8,128)S(1)} %get-tuple-element.34, f32[32,512]{1,0:T(8,128)S(1)} %fusion.5, f32[32,512]{1,0:T(8,128)S(1)} %get-tuple-element.32, f32[32,512,512]{2,1,0:T(8,128)} %get-tuple-element.33, pred[512,512]{0,1:T(8,128)(4,1)S(1)} %iota_compare_fusion), kind=kLoop, calls=%fused_computation.11 | loop fusion | flops 67108864 | bytes 84344832 | tf_op jit(solution)/shard_map/reshape.16
  338.2 11.9 %convert_bitcast_fusion.2 = bf16[32,512,1,128]{1,3,0,2:T(8,128)(2,1)} fusion(bf16[32,512,128]{2,1,0:T(8,128)(2,1)} %bitcast.270, bf16[32,512,512]{1,2,0:T(8,128)(2,1)} %fusion.7), kind=kOutput, calls=%fused_computation.77 | convolution fusion | flops 2149580800 | bytes 25165824 | tf_op jit(solution)/shard_map/bkgqs,bqkgd->bskd/dot_general | solution.py:55
  350.0 8.1 copy.246
  358.1 4.4 all-to-all-start.6
  362.6 18.8 %convert_bitcast_fusion.1 = bf16[32,512,1,128]{1,3,0,2:T(8,128)(2,1)} fusion(bf16[32,512,128]{2,1,0:T(8,128)(2,1)} %bitcast.293, f32[32,512]{1,0:T(8,128)S(1)} %fusion.5, f32[32,512]{1,0:T(8,128)S(1)} %get-tuple-element.32, f32[32,512,512]{2,1,0:T(8,128)} %get-tuple-element.33, pred[512,512]{0,1:T(8,128)(4,1)S(1)} %iota_compare_fusion), kind=kOutput, calls=%fused_computation.72 | convolution fusion | flops 2191523840 | bytes 42336256 | tf_op jit(solution)/shard_map/bkgqs,bqkgd->bskd/dot_general | solution.py:56
  381.3 10.4 %convert_bitcast_fusion.3 = bf16[32,512,1,128]{1,3,0,2:T(8,128)(2,1)} fusion(bf16[32,512,128]{2,1,0:T(8,128)(2,1)S(1)} %bitcast.272, bf16[32,512,512]{1,2,0:T(8,128)(2,1)} %fusion.7), kind=kOutput, calls=%fused_computation.78 | convolution fusion | flops 2149580800 | bytes 25165824 | tf_op jit(solution)/shard_map/bkgqs,bskd->bqkgd/dot_general | solution.py:54
  391.8 7.9 copy.239
  399.7 16.4 %all-to-all-done.6 = bf16[32,512,1,128]{3,0,2,1:T(8,128)(2,1)} async-done(((bf16[32,512,1,128]{3,0,2,1:T(8,128)(2,1)}), bf16[32,512,1,128]{3,0,2,1:T(8,128)(2,1)}, u32[]{:S(2)}, u32[]{:S(2)}) %all-to-all-start.6) | async-done | bytes 4194336 | tf_op jit(solution)/shard_map/all_to_all | solution.py:100
  416.0 4.8 all-to-all-start.5
  420.9 17.9 %convert_bitcast_fusion.5 = bf16[32,512,1,128]{1,3,0,2:T(8,128)(2,1)} fusion(bf16[32,512,128]{2,1,0:T(8,128)(2,1)} %bitcast.291, f32[32,512]{1,0:T(8,128)S(1)} %fusion.5, f32[32,512]{1,0:T(8,128)S(1)} %get-tuple-element.32, f32[32,512,512]{2,1,0:T(8,128)} %get-tuple-element.33, pred[512,512]{0,1:T(8,128)(4,1)S(1)} %iota_compare_fusion), kind=kOutput, calls=%fused_computation.80 | convolution fusion | flops 2191523840 | bytes 42336256 | tf_op jit(solution)/shard_map/bkgqs,bskd->bqkgd/dot_general | solution.py:41
  438.8 7.9 copy.253
  446.7 7.8 copy.232
  454.6 5.8 copy.247
  460.4 5.6 reduce_sum.153
  466.0 4.2 convert_element_type.138
  470.2 4.2 all-to-all-done.5
  474.4 4.6 all-to-all-start.7
  479.0 4.8 multiply_add_fusion.3
  483.9 6.7 copy.240
  490.7 4.3 multiply_reduce_fusion.1
  496.3 7.4 multiply_add_fusion.1
  503.7 12.0 %multiply_reduce_fusion = (f32[128]{0:T(128)}, f32[32,32,16]{1,2,0:T(8,128)S(1)}) fusion(f32[32,32,16]{1,2,0:T(8,128)S(1)} %copy-done.14, f32[32,32,16,64]{3,1,2,0:T(8,128)} %get-tuple-element.23, f32[32,32,16,64]{3,1,2,0:T(8,128)} %get-tuple-element.22, f32[128]{0:T(128)S(1)} %copy-done.40, f32[32,32,2048]{2,1,0:T(8,128)S(1)} %bitcast.266), kind=kLoop, calls=%fused_computation.26 | loop fusion | flops 14663552 | bytes 16909312 | tf_op jit(solution)/shard_map/transpose(jvp())/reduce_sum | solution.py:12
  515.9 4.4 fusion.51
  520.2 12.2 %all-to-all-done.7 = bf16[32,512,1,128]{3,0,2,1:T(8,128)(2,1)} async-done(((bf16[32,512,1,128]{3,0,2,1:T(8,128)(2,1)}), bf16[32,512,1,128]{3,0,2,1:T(8,128)(2,1)}, u32[]{:S(2)}, u32[]{:S(2)}) %all-to-all-start.7) | async-done | bytes 4194336 | tf_op jit(solution)/shard_map/all_to_all | solution.py:101
  532.5 4.4 all-to-all-start.3
  537.2 5.8 copy.254
  543.0 5.6 reduce_sum.155
  548.6 7.0 convolution_bitcast_fusion.3
  555.7 4.7 convolution_bitcast_fusion.2
  562.5 7.5 fusion.27
  572.0 7.2 convolution_bitcast_fusion.1
  579.2 11.2 %all-to-all-done.3 = bf16[32,512,1,128]{3,0,2,1:T(8,128)(2,1)} async-done(((bf16[32,512,1,128]{3,0,2,1:T(8,128)(2,1)}), bf16[32,512,1,128]{3,0,2,1:T(8,128)(2,1)}, u32[]{:S(2)}, u32[]{:S(2)}) %all-to-all-start.3) | async-done | bytes 4194336 | tf_op jit(solution)/shard_map/all_to_all | solution.py:93
  594.2 4.0 copy.234
  598.2 7.7 reshape.273
  605.9 10.8 %convolution_bitcast_fusion = f32[2048,1024]{1,0:T(8,128)} fusion(bf16[32,32,2048]{2,1,0:T(8,128)(2,1)} %reshape.273, bf16[32,32,1024]{2,1,0:T(8,128)(2,1)} %param.17), kind=kOutput, calls=%fused_computation.42 | convolution fusion | flops 4294967296 | bytes 14680064 | tf_op jit(solution)/shard_map/bse,bsd->ed/dot_general | solution.py:96
  616.8 4.7 fusion.53
  621.5 4.5 fusion.30
  626.1 5.0 fusion.20
  631.1 34.5 %all-reduce.4 = (f32[1024]{0:T(1024)}, f32[128]{0:T(128)}, f32[128]{0:T(128)}) all-reduce(f32[1024]{0:T(1024)S(1)} %get-tuple-element.13, f32[128]{0:T(128)S(1)} %copy-done.43, f32[128]{0:T(128)S(1)} %copy-done.44), channel_id=1, replica_groups=mesh['sp'=16] {'sp'}, use_global_device_ids=true, to_apply=%region_16.17 | all-reduce | flops 1280 | bytes 10240 | tf_op jit(solution)/shard_map/psum | solution.py:115
  665.7 5.2 fusion.23
  672.9 5.7 fusion.25
  678.6 188.7 %all-reduce.8.cloned.1.call-done = (f32[1024,2048]{1,0:T(8,128)}, f32[1024,1024]{1,0:T(8,128)}, f32[1024,1024]{1,0:T(8,128)}, f32[2048,1024]{1,0:T(8,128)}) async-done(((f32[1024,2048]{1,0:T(8,128)}, f32[1024,1024]{1,0:T(8,128)}, f32[1024,1024]{1,0:T(8,128)}, f32[2048,1024]{1,0:T(8,128)}), (f32[1024,2048]{1,0:T(8,128)}, f32[1024,1024]{1,0:T(8,128)}, f32[1024,1024]{1,0:T(8,128)}, ...) | async-done | bytes 25165840 | tf_op jit(solution)/shard_map/psum | solution.py:115
  867.3 8.0 copy.321
  (153 shorter events, 60.8 us)
Async XLA Ops:
  7.2 35.6 %copy-start = (bf16[1024,1024]{1,0:T(8,128)(2,1)S(1)}, bf16[1024,1024]{1,0:T(8,128)(2,1)}, u32[]{:S(2)}) copy-start(bf16[1024,1024]{1,0:T(8,128)(2,1)} %param.12) | copy-start | bytes 6291460
  10.0 153.6 %copy-start.35 = (f32[32,32]{1,0:T(8,128)}, f32[32,32]{1,0:T(8,128)S(1)}, u32[]{:S(2)}) copy-start(f32[32,32]{1,0:T(8,128)S(1)} %fusion.80) | copy-start | bytes 12292
  17.1 3.5 copy-start.1
  20.6 2.5 copy-start.39
  23.0 5.4 copy-start.21
  23.0 5.4 copy-start.13
  28.6 25.9 %copy-start.29 = (f32[32,64]{1,0:T(8,128)}, f32[32,64]{1,0:T(8,128)S(1)}, u32[]{:S(2)}) copy-start(f32[32,64]{1,0:T(8,128)S(1)} %get-tuple-element.30) | copy-start | bytes 24580
  28.6 25.9 %copy-start.31 = (f32[32,64]{1,0:T(8,128)}, f32[32,64]{1,0:T(8,128)S(1)}, u32[]{:S(2)}) copy-start(f32[32,64]{1,0:T(8,128)S(1)} %get-tuple-element.31) | copy-start | bytes 24580
  37.2 5.7 copy-start.41
  37.2 59.1 %all-to-all-start.2 = ((bf16[32,32,16,128]{3,1,0,2:T(8,128)(2,1)}), bf16[32,32,16,128]{3,1,0,2:T(8,128)(2,1)}, u32[]{:S(2)}, u32[]{:S(2)}) async-start(bf16[32,32,16,128]{3,1,0,2:T(8,128)(2,1)} %copy.228), calls=%async_computation.2 | async-start | bytes 8388608 | tf_op jit(solution)/shard_map/all_to_all | solution.py:89
  46.8 2.0 copy-start.3
  48.8 2.1 copy-start.37
  50.2 4.3 copy-start.27
  100.8 58.4 %all-to-all-start.1 = ((bf16[32,32,16,128]{3,1,0,2:T(8,128)(2,1)}), bf16[32,32,16,128]{3,1,0,2:T(8,128)(2,1)}, u32[]{:S(2)}, u32[]{:S(2)}) async-start(bf16[32,32,16,128]{3,1,0,2:T(8,128)(2,1)} %bitcast.282), calls=%async_computation.1 | async-start | bytes 8388608 | tf_op jit(solution)/shard_map/all_to_all | solution.py:90
  159.2 57.9 %all-to-all-start.4 = ((bf16[32,32,16,128]{3,1,0,2:T(8,128)(2,1)}), bf16[32,32,16,128]{3,1,0,2:T(8,128)(2,1)}, u32[]{:S(2)}, u32[]{:S(2)}) async-start(bf16[32,32,16,128]{3,1,0,2:T(8,128)(2,1)} %bitcast.280), calls=%async_computation.4 | async-start | bytes 8388608 | tf_op jit(solution)/shard_map/all_to_all | solution.py:97
  221.6 58.1 %all-to-all-start = ((bf16[32,32,16,128]{3,1,0,2:T(8,128)(2,1)}), bf16[32,32,16,128]{3,1,0,2:T(8,128)(2,1)}, u32[]{:S(2)}, u32[]{:S(2)}) async-start(bf16[32,32,16,128]{3,1,0,2:T(8,128)(2,1)} %bitcast.281), calls=%async_computation | async-start | bytes 8388608 | tf_op jit(solution)/shard_map/all_to_all | solution.py:91
  283.2 26.8 %copy-start.18 = (bf16[32,32,16,128]{3,1,2,0:T(8,128)(2,1)}, bf16[32,32,16,128]{3,1,2,0:T(8,128)(2,1)S(1)}, u32[]{:S(2)}) copy-start(bf16[32,32,16,128]{3,1,2,0:T(8,128)(2,1)S(1)} %copy.221) | copy-start | bytes 12582916
  358.1 57.9 %all-to-all-start.6 = ((bf16[32,512,1,128]{3,0,2,1:T(8,128)(2,1)}), bf16[32,512,1,128]{3,0,2,1:T(8,128)(2,1)}, u32[]{:S(2)}, u32[]{:S(2)}) async-start(bf16[32,512,1,128]{3,0,2,1:T(8,128)(2,1)} %copy.246), calls=%async_computation.6 | async-start | bytes 8388608 | tf_op jit(solution)/shard_map/all_to_all | solution.py:100
  362.6 18.8 %copy-start.2 = (bf16[32,16,32,1,128]{4,2,1,0,3:T(8,128)(2,1)S(1)}, bf16[32,16,32,1,128]{4,2,1,0,3:T(8,128)(2,1)}, u32[]{:S(2)}) copy-start(bf16[32,16,32,1,128]{4,2,1,0,3:T(8,128)(2,1)} %copy.225) | copy-start | bytes 12582916
  416.0 58.3 %all-to-all-start.5 = ((bf16[32,512,1,128]{3,0,2,1:T(8,128)(2,1)}), bf16[32,512,1,128]{3,0,2,1:T(8,128)(2,1)}, u32[]{:S(2)}, u32[]{:S(2)}) async-start(bf16[32,512,1,128]{3,0,2,1:T(8,128)(2,1)} %copy.239), calls=%async_computation.5 | async-start | bytes 8388608 | tf_op jit(solution)/shard_map/all_to_all | solution.py:99
  470.2 8.8 copy-start.30
  470.2 8.8 copy-start.32
  474.4 58.1 %all-to-all-start.7 = ((bf16[32,512,1,128]{3,0,2,1:T(8,128)(2,1)}), bf16[32,512,1,128]{3,0,2,1:T(8,128)(2,1)}, u32[]{:S(2)}, u32[]{:S(2)}) async-start(bf16[32,512,1,128]{3,0,2,1:T(8,128)(2,1)} %copy.253), calls=%async_computation.7 | async-start | bytes 8388608 | tf_op jit(solution)/shard_map/all_to_all | solution.py:101
  483.8 6.8 copy-start.6
  483.8 6.8 copy-start.8
  483.9 6.8 copy-start.4
  483.9 6.8 copy-start.24
  483.9 6.8 copy-start.38
  490.7 4.3 copy-start.28
  495.0 8.7 slice-start
  496.2 7.5 slice-start.1
  496.2 7.5 copy-start.14
  496.2 7.4 copy-start.40
  503.7 12.1 %copy-start.22 = (f32[32,32,16]{1,2,0:T(8,128)S(1)}, f32[32,32,16]{1,2,0:T(8,128)}, u32[]{:S(2)}) copy-start(f32[32,32,16]{1,2,0:T(8,128)} %copy-done.21) | copy-start | bytes 196612
  503.7 12.2 %copy-start.5 = (f32[32,32,1024]{2,1,0:T(8,128)S(1)}, f32[32,32,1024]{2,1,0:T(8,128)}, u32[]{:S(2)}) copy-start(f32[32,32,1024]{2,1,0:T(8,128)} %copy-done.3) | copy-start | bytes 12582916
  503.7 12.1 %copy-start.7 = (f32[32,32,8,64]{3,1,2,0:T(8,128)S(1)}, f32[32,32,8,64]{3,1,2,0:T(8,128)}, u32[]{:S(2)}) copy-start(f32[32,32,8,64]{3,1,2,0:T(8,128)} %copy-done.6) | copy-start | bytes 6291460
  503.7 12.1 %copy-start.9 = (f32[32,32,8,64]{3,1,2,0:T(8,128)S(1)}, f32[32,32,8,64]{3,1,2,0:T(8,128)}, u32[]{:S(2)}) copy-start(f32[32,32,8,64]{3,1,2,0:T(8,128)} %copy-done.8) | copy-start | bytes 6291460
  532.5 57.9 %all-to-all-start.3 = ((bf16[32,512,1,128]{3,0,2,1:T(8,128)(2,1)}), bf16[32,512,1,128]{3,0,2,1:T(8,128)(2,1)}, u32[]{:S(2)}, u32[]{:S(2)}) async-start(bf16[32,512,1,128]{3,0,2,1:T(8,128)(2,1)} %copy.232), calls=%async_computation.3 | async-start | bytes 8388608 | tf_op jit(solution)/shard_map/all_to_all | solution.py:93
  536.9 330.4 %all-reduce.8.cloned.1.call-start = ((), (), s32[]{:S(2)}) async-start(), calls=%async_computation.8 | async-start | bytes 50331648 | tf_op jit(solution)/shard_map/psum | solution.py:115
  543.0 5.6 copy-start.36
  543.0 5.6 copy-start.42
  548.6 7.1 copy-start.10
  548.6 7.1 copy-start.25
  548.6 11.8 %slice-start.2 = ((s8[8388608]{0:T(1024)(128)(4,1)}), s8[4194304]{0:T(1024)(128)(4,1)S(1)}, s32[]{:S(2)}) async-start(s8[8388608]{0:T(1024)(128)(4,1)} %bitcast.267), calls=%async_computation.11 | async-start | bytes 8388608
  548.6 11.8 %slice-start.4 = ((s8[8388608]{0:T(1024)(128)(4,1)}), s8[4194304]{0:T(1024)(128)(4,1)S(1)}, s32[]{:S(2)}) async-start(s8[8388608]{0:T(1024)(128)(4,1)} %bitcast.273), calls=%async_computation.13 | async-start | bytes 8388608
  548.6 11.8 %slice-start.6 = ((s8[8388608]{0:T(1024)(128)(4,1)}), s8[4194304]{0:T(1024)(128)(4,1)S(1)}, s32[]{:S(2)}) async-start(s8[8388608]{0:T(1024)(128)(4,1)} %bitcast.275), calls=%async_computation.15 | async-start | bytes 8388608
  555.7 4.7 slice-start.3
  555.7 4.9 slice-start.5
  555.7 6.8 slice-start.7
  569.9 2.1 copy-start.19
  616.7 4.8 copy-start.20
  616.7 4.8 copy-start.45
  621.5 4.6 copy-start.11
  621.5 4.6 copy-start.26
  626.1 5.0 copy-start.43
  626.1 5.0 copy-start.44
  626.1 39.5 %copy-start.34 = (f32[32,32]{1,0:T(8,128)S(1)}, f32[32,32]{1,0:T(8,128)}, u32[]{:S(2)}) copy-start(f32[32,32]{1,0:T(8,128)} %copy-done.33) | copy-start | bytes 12292
  665.6 5.3 copy-start.12
  665.6 6.0 copy-start.17
  665.6 7.2 copy-start.46
  867.3 8.0 copy-start.16
  875.3 3.7 copy-start.15
  875.3 5.8 slice-start.8
  879.0 4.2 slice-start.9
  (2 other events, 1.3 us)
Sparse Core Ops, SparseCore 0:
  616.9 250.3 all-reduce.7
where the time goes:
time: 904 us; the launch traced here: 894 us
  waiting for transfers between devices  366 us (40%)
  matrix products  175 us (19%)
  local copies, waits for them, and re-layouts  137 us (15%)
  other arithmetic  128 us (14%)
  starting transfers between devices  38.2 us (4%)
  blocking collectives  34.5 us (4%)
  between operations  15.1 us (2%)
    psum x1, waiting for transfers between devices, local_step(): lax.psum(d_wq, 'sp')  189 us
    all_to_all x1, waiting for transfers between devices, local_step(): k_here = lax.all_to_all(k_rep, 'sp', 2, 1, tiled=True)  43.1 us
    all_to_all x1, waiting for transfers between devices, local_step(): q_here = lax.all_to_all(q_rot.astype(jnp.bfloat16), 'sp', 2, 1, tiled=True)  37.3 us
    all_to_all x1, waiting for transfers between devices, local_step(): d_o_here = lax.all_to_all(d_attn.reshape(q_shape), 'sp', 2, 1, tiled=True)  36.2 us
    psum x1, blocking collectives, local_step(): lax.psum(d_ngain, 'sp')  34.5 us
    another operation x3, other arithmetic  32.7 us
    unnamed x120, local copies, waits for them, and re-layouts  32.4 us
    dot_general x1, matrix products, core_backward(): jnp.einsum('bqkgd,bskd->bkgqs', d_grouped, v_part, preferred_element_type...  26.8 us
  transfers between devices with their start and end apart: 9, of which 9 were waited for; matrix products, arithmetic and copies ran while one was open for 30% of the time, Pallas kernels for 0%

commit v1 on v0

v1 whole, which is shorter than its diff:
```python
import math
import jax
import jax.numpy as jnp
from jax import lax
from jax.experimental import pallas as pl
from jax.experimental.pallas import tpu as pltpu
from jax.sharding import PartitionSpec as P

ROPE_BASE = 1000000.0
NORM_EPS = 1e-6
LOG2E = 1.4426950408889634
F32 = jnp.float32
BF16 = jnp.bfloat16
QBLK = 256
VMEM_LIMIT = 60 * 1024 * 1024


def dot(a, b, ca, cb):
    return lax.dot_general(a, b, (((ca,), (cb,)), ((), ())), preferred_element_type=F32)


def rope_tables(n_pos, head_dim):
    half_dim = head_dim // 2
    inv_freq = jnp.exp(jnp.arange(half_dim).astype(F32) * (-2.0 * math.log(ROPE_BASE) / head_dim))
    angles = jnp.arange(n_pos).astype(F32)[:, None] * inv_freq[None, :]
    cos, sin = jnp.cos(angles), jnp.sin(angles)
    return jnp.concatenate([cos, cos], axis=-1), jnp.concatenate([-sin, sin], axis=-1)


def norm_rope(raw, gain, cos, sin):
    inv = lax.rsqrt(jnp.mean(raw * raw, axis=-1, keepdims=True) + NORM_EPS)
    normed = raw * inv * gain
    return normed * cos + pltpu.roll(normed, raw.shape[-1] // 2, 1) * sin


def norm_rope_back(d_rot, raw, gain, cos, sin):
    inv = lax.rsqrt(jnp.mean(raw * raw, axis=-1, keepdims=True) + NORM_EPS)
    unit = raw * inv
    d_normed = d_rot * cos - pltpu.roll(d_rot, raw.shape[-1] // 2, 1) * sin
    d_gain = jnp.sum(d_normed * unit, axis=0, keepdims=True)
    d_unit = d_normed * gain
    d_raw = inv * (d_unit - unit * jnp.mean(d_unit * unit, axis=-1, keepdims=True))
    return d_raw, d_gain


def causal_mask_t(scores_t, first_q):
    n_key, n_q = scores_t.shape
    key = lax.broadcasted_iota(jnp.int32, (n_q, n_q), 0)
    query = lax.broadcasted_iota(jnp.int32, (n_q, n_q), 1)
    diag = jnp.where(query >= key, scores_t[first_q:], -1e30)
    if first_q == 0:
        return diag
    return jnp.concatenate([scores_t[:first_q], diag], axis=0)


def fwd_kernel(x_ref, gain_ref, wq_ref, wk_ref, wv_ref, qg_ref, kg_ref, cos_ref, sin_ref,
               h_ref, qraw_ref, kraw_ref, qrot_ref, krot_ref, v_ref, o_ref, lse_ref):
    n_src, _, n_loc, dim = x_ref.shape
    n_pos = n_src * n_loc
    head_dim = qg_ref.shape[-1]
    group = wq_ref.shape[1] // head_dim

    @pl.when(pl.program_id(1) == 0)
    def _():
        x = x_ref[:, 0].reshape(n_pos, dim).astype(F32)
        inv = lax.rsqrt(jnp.mean(x * x, axis=-1, keepdims=True) + NORM_EPS)
        h_ref[:, 0] = (x * inv * gain_ref[...]).astype(BF16).reshape(n_src, n_loc, dim)

    h = h_ref[:, 0].reshape(n_pos, dim)
    cos, sin = cos_ref[...], sin_ref[...]
    q_raw = dot(h, wq_ref[...], 1, 0).astype(BF16)
    k_raw = dot(h, wk_ref[...], 1, 0).astype(BF16)
    v = dot(h, wv_ref[...], 1, 0).astype(BF16)
    qraw_ref[0] = q_raw
    kraw_ref[0] = k_raw
    v_ref[0] = v
    k_rot = norm_rope(k_raw.astype(F32), kg_ref[...], cos, sin).astype(BF16)
    krot_ref[0] = k_rot
    scale = head_dim ** -0.5 * LOG2E
    for j in range(group):
        cols = slice(j * head_dim, (j + 1) * head_dim)
        q_rot = norm_rope(q_raw[:, cols].astype(F32), qg_ref[...], cos, sin).astype(BF16)
        qrot_ref[0, :, cols] = q_rot
        for first in range(0, n_pos, QBLK):
            n_key = first + QBLK
            scores = causal_mask_t(dot(k_rot[:n_key], q_rot[first:n_key], 1, 1) * scale, first)
            top = jnp.max(scores, axis=0, keepdims=True)
            e = jnp.exp2(scores - top)
            total = jnp.sum(e, axis=0, keepdims=True)
            prob = (e * (1.0 / total)).astype(BF16)
            lse_ref[0, 0, j:j + 1, first:n_key] = top + jnp.log2(total)
            o_blk = dot(prob, v[:n_key], 0, 0).astype(BF16)
            o_ref[first // n_loc:n_key // n_loc, 0, :, cols] = o_blk.reshape(QBLK // n_loc, n_loc, head_dim)


def bwd_kernel(dy_ref, wo_ref, qraw_ref, kraw_ref, qrot_ref, krot_ref, v_ref, lse_ref, qg_ref, kg_ref, cos_ref, sin_ref,
               dq_ref, dk_ref, dv_ref, dqg_ref, dkg_ref):
    n_src, _, n_loc, dim = dy_ref.shape
    n_pos = n_src * n_loc
    head_dim = qg_ref.shape[-1]
    group = wo_ref.shape[0] // head_dim

    @pl.when((pl.program_id(0) == 0) & (pl.program_id(1) == 0))
    def _():
        dqg_ref[...] = jnp.zeros_like(dqg_ref)
        dkg_ref[...] = jnp.zeros_like(dkg_ref)

    cos, sin = cos_ref[...], sin_ref[...]
    scale = head_dim ** -0.5
    d_o = dot(dy_ref[:, 0].reshape(n_pos, dim), wo_ref[...], 1, 1).astype(BF16)
    k_rot, v = krot_ref[0], v_ref[0]
    dk_sum = [jnp.zeros((QBLK, head_dim), F32) for _ in range(n_pos // QBLK)]
    dv_sum = [jnp.zeros((QBLK, head_dim), F32) for _ in range(n_pos // QBLK)]
    for j in range(group):
        cols = slice(j * head_dim, (j + 1) * head_dim)
        dq_parts = []
        for first in range(0, n_pos, QBLK):
            n_key = first + QBLK
            q_blk = qrot_ref[0, first:n_key, cols]
            do_blk = d_o[first:n_key, cols]
            scores = causal_mask_t(dot(k_rot[:n_key], q_blk, 1, 1) * (scale * LOG2E), first)
            prob = jnp.exp2(scores - lse_ref[0, 0, j:j + 1, first:n_key])
            d_prob = dot(v[:n_key], do_blk, 1, 1)
            inner = jnp.sum(prob * d_prob, axis=0, keepdims=True)
            d_scores = (prob * (d_prob - inner) * scale).astype(BF16)
            dv_blk = dot(prob.astype(BF16), do_blk, 1, 0)
            dk_blk = dot(d_scores, q_blk, 1, 0)
            for i in range(n_key // QBLK):
                dv_sum[i] += dv_blk[i * QBLK:(i + 1) * QBLK]
                dk_sum[i] += dk_blk[i * QBLK:(i + 1) * QBLK]
            dq_parts.append(dot(d_scores, k_rot[:n_key], 0, 0))
        dq = jnp.concatenate(dq_parts, axis=0).astype(BF16).astype(F32)
        dq_raw, d_gain = norm_rope_back(dq, qraw_ref[0, :, cols].astype(F32), qg_ref[...], cos, sin)
        dq_ref[:, 0, :, cols] = dq_raw.astype(BF16).reshape(n_src, n_loc, head_dim)
        dqg_ref[...] += d_gain
    dk = jnp.concatenate(dk_sum, axis=0).astype(BF16).astype(F32)
    dk_raw, d_gain = norm_rope_back(dk, kraw_ref[0].astype(F32), kg_ref[...], cos, sin)
    dk_ref[:, 0] = dk_raw.astype(BF16).reshape(n_src, n_loc, head_dim)
    dkg_ref[...] += d_gain
    dv_ref[:, 0] = jnp.concatenate(dv_sum, axis=0).astype(BF16).reshape(n_src, n_loc, head_dim)


def attention_fwd(x, norm_gain, w_q, w_k, w_v, q_gain, k_gain, cos, sin):
    n_src, rows, n_loc, dim = x.shape
    n_pos, head_dim = cos.shape
    kv_heads = w_k.shape[1] // head_dim
    group = w_q.shape[1] // w_k.shape[1]
    qw = group * head_dim
    seq = lambda width: pl.BlockSpec((1, n_pos, width), lambda r, g: (r, 0, g))
    const = lambda shape: pl.BlockSpec(shape, lambda r, g: (0, 0))
    weight = lambda width: pl.BlockSpec((dim, width), lambda r, g: (0, g))
    return pl.pallas_call(
        fwd_kernel,
        grid=(rows, kv_heads),
        in_specs=[
            pl.BlockSpec((n_src, 1, n_loc, dim), lambda r, g: (0, r, 0, 0)), const((1, dim)),
            weight(qw), weight(head_dim), weight(head_dim), const((1, head_dim)), const((1, head_dim)),
            const((n_pos, head_dim)), const((n_pos, head_dim))],
        out_specs=[
            pl.BlockSpec((n_src, 1, n_loc, dim), lambda r, g: (0, r, 0, 0)),
            seq(qw), seq(head_dim), seq(qw), seq(head_dim), seq(head_dim),
            pl.BlockSpec((n_src, 1, n_loc, qw), lambda r, g: (0, r, 0, g)),
            pl.BlockSpec((1, 1, group, n_pos), lambda r, g: (r, g, 0, 0))],
        out_shape=[
            jax.ShapeDtypeStruct(x.shape, BF16),
            jax.ShapeDtypeStruct((rows, n_pos, kv_heads * qw), BF16),
            jax.ShapeDtypeStruct((rows, n_pos, kv_heads * head_dim), BF16),
            jax.ShapeDtypeStruct((rows, n_pos, kv_heads * qw), BF16),
            jax.ShapeDtypeStruct((rows, n_pos, kv_heads * head_dim), BF16),
            jax.ShapeDtypeStruct((rows, n_pos, kv_heads * head_dim), BF16),
            jax.ShapeDtypeStruct((n_src, rows, n_loc, kv_heads * qw), BF16),
            jax.ShapeDtypeStruct((rows, kv_heads, group, n_pos), F32)],
        compiler_params=pltpu.CompilerParams(
            dimension_semantics=('arbitrary', 'arbitrary'), vmem_limit_bytes=VMEM_LIMIT),
        cost_estimate=pl.CostEstimate(flops=12 * 10**9, bytes_accessed=50 * 10**6, transcendentals=0),
        name='attn_fwd',
    )(x, norm_gain[None], w_q, w_k, w_v, q_gain[None], k_gain[None], cos, sin)


def attention_bwd(d_y, w_o, q_raw, k_raw, q_rot, k_rot, v, lse, q_gain, k_gain, cos, sin):
    n_src, rows, n_loc, dim = d_y.shape
    n_pos, head_dim = cos.shape
    _, kv_heads, group, _ = lse.shape
    qw = group * head_dim
    seq = lambda width: pl.BlockSpec((1, n_pos, width), lambda r, g: (r, 0, g))
    const = lambda shape: pl.BlockSpec(shape, lambda r, g: (0, 0))
    out = lambda width: pl.BlockSpec((n_src, 1, n_loc, width), lambda r, g: (0, r, 0, g))
    return pl.pallas_call(
        bwd_kernel,
        grid=(rows, kv_heads),
        in_specs=[
            pl.BlockSpec((n_src, 1, n_loc, dim), lambda r, g: (0, r, 0, 0)),
            pl.BlockSpec((qw, dim), lambda r, g: (g, 0)),
            seq(qw), seq(head_dim), seq(qw), seq(head_dim), seq(head_dim),
            pl.BlockSpec((1, 1, group, n_pos), lambda r, g: (r, g, 0, 0)),
            const((1, head_dim)), const((1, head_dim)), const((n_pos, head_dim)), const((n_pos, head_dim))],
        out_specs=[out(qw), out(head_dim), out(head_dim), const((1, head_dim)), const((1, head_dim))],
        out_shape=[
            jax.ShapeDtypeStruct((n_src, rows, n_loc, kv_heads * qw), BF16),
            jax.ShapeDtypeStruct((n_src, rows, n_loc, kv_heads * head_dim), BF16),
            jax.ShapeDtypeStruct((n_src, rows, n_loc, kv_heads * head_dim), BF16),
            jax.ShapeDtypeStruct((1, head_dim), F32),
            jax.ShapeDtypeStruct((1, head_dim), F32)],
        compiler_params=pltpu.CompilerParams(
            dimension_semantics=('arbitrary', 'arbitrary'), vmem_limit_bytes=VMEM_LIMIT),
        cost_estimate=pl.CostEstimate(flops=14 * 10**9, bytes_accessed=50 * 10**6, transcendentals=0),
        name='attn_bwd',
    )(d_y, w_o, q_raw, k_raw, q_rot, k_rot, v, lse, q_gain[None], k_gain[None], cos, sin)


def solution(mesh):
    n_dev = mesh.shape['sp']
    seq_spec = P(None, 'sp', None)
    replicated = P()

    def local_step(hidden, norm_gain, w_q, w_k, w_v, q_gain, k_gain, w_o, d_out):
        n_batch, n_loc, dim = hidden.shape
        head_dim = q_gain.shape[0]
        rows = n_batch // n_dev
        tokens = rows * n_loc * n_dev
        cos, sin = rope_tables(n_loc * n_dev, head_dim)

        def exchange(a):
            return lax.all_to_all(a.reshape(n_dev, rows, n_loc, dim), 'sp', 0, 0, tiled=True)

        x = exchange(hidden)
        d_y = exchange(d_out)
        h, q_raw, k_raw, q_rot, k_rot, v, o, lse = attention_fwd(x, norm_gain, w_q, w_k, w_v, q_gain, k_gain, cos, sin)
        o = o.reshape(tokens, -1)
        h = h.reshape(tokens, dim)
        dy_flat = d_y.reshape(tokens, dim)
        x_f = x.reshape(tokens, dim).astype(F32)
        d_wo = lax.psum(dot(o, dy_flat, 0, 0), 'sp')
        y = (x_f + dot(o, w_o, 1, 0)).astype(BF16)
        y_out = exchange(y).reshape(n_batch, n_loc, dim)
        dq, dk, dv, d_qg, d_kg = attention_bwd(d_y, w_o, q_raw, k_raw, q_rot, k_rot, v, lse, q_gain, k_gain, cos, sin)
        dq = dq.reshape(tokens, -1)
        dk = dk.reshape(tokens, -1)
        dv = dv.reshape(tokens, -1)
        d_normed = dot(dq, w_q, 1, 1) + dot(dk, w_k, 1, 1) + dot(dv, w_v, 1, 1)
        inv = lax.rsqrt(jnp.mean(x_f * x_f, axis=-1, keepdims=True) + NORM_EPS)
        unit = x_f * inv
        d_ng = jnp.sum(d_normed * unit, axis=0)
        d_unit = d_normed * norm_gain
        d_x = inv * (d_unit - unit * jnp.mean(d_unit * unit, axis=-1, keepdims=True))
        d_hidden = exchange((dy_flat.astype(F32) + d_x).astype(BF16)).reshape(n_batch, n_loc, dim)
        d_wq = dot(h, dq, 0, 0)
        d_wk = dot(h, dk, 0, 0)
        d_wv = dot(h, dv, 0, 0)
        late, d_wo = lax.optimization_barrier(((d_wq, d_wk, d_wv, d_ng, d_qg[0], d_kg[0]), d_wo))
        d_wq, d_wk, d_wv, d_ng, d_qg, d_kg = lax.psum(late, 'sp')
        return y_out, d_hidden, d_wq, d_wk, d_wv, d_wo, d_ng, d_qg, d_kg

    return jax.shard_map(local_step, mesh=mesh, in_specs=(seq_spec, replicated, replicated, replicated, replicated, replicated, replicated, replicated, seq_spec), out_specs=(seq_spec, seq_spec, replicated, replicated, replicated, replicated, replicated, replicated, replicated), check_vma=False)
```

time: 904 us -> 547 us (0.61); the launches traced: 894 us -> 546 us
  matrix products: 175 us -> 52.7 us
  other arithmetic: 128 us -> 7 us
  local copies, waits for them, and re-layouts: 137 us -> 25.1 us
  Pallas kernels: 0 us -> 98.9 us
  waiting for transfers between devices: 366 us -> 300 us
  starting transfers between devices: 38.2 us -> 15.7 us
    dot_general x18 -> x8, matrix products: 175 us -> 52.7 us  [dot(): lax.dot_general(a, b, (((ca,), (cb,)), ((), ())), preferred_element_type=...]
    pallas_call x0 -> x2, Pallas kernels: none -> 98.9 us  [the longest x1 54.6 us: attention_bwd(): pl.pallas_call(bwd_kernel, grid=(rows, kv_heads), in_specs=[pl.BlockSpec(...]
    all_to_all x8 -> x4, waiting for transfers between devices: 177 us -> 112 us  [exchange(): lax.all_to_all(a.reshape(n_dev, rows, n_loc, dim), 'sp', 0, 0, tiled=True)]
    reduce_sum x8 -> x1, other arithmetic: 47.7 us -> 0.49 us  [local_step(): inv = lax.rsqrt(jnp.mean(x_f * x_f, axis=-1, keepdims=True) + NORM_EPS)]
    all_to_all x9 -> x0, local copies, waits for them, and re-layouts: 45.9 us -> none  [the longest x2 7.77 us: local_step(): lax.all_to_all(o_here, 'sp', 1, 2, tiled=True)]
    another operation x3 -> x0, other arithmetic: 32.7 us -> none
    reshape x5 -> x0, local copies, waits for them, and re-layouts: 28.2 us -> none  [the longest x1 7.92 us: core_backward(): d_q.astype(jnp.bfloat16).reshape(n_batch, n_pos, q_heads, head_dim)]
    all_to_all x8 -> x4, starting transfers between devices: 37.9 us -> 15.4 us  [exchange(): lax.all_to_all(a.reshape(n_dev, rows, n_loc, dim), 'sp', 0, 0, tiled=True)]
  transfers between devices with their start and end apart: 9 -> 6, of which waited for: 9 -> 5; matrix products, arithmetic and copies ran while one was open for 30% -> 7% of each run, Pallas kernels for 0% -> 8%
where the time goes in v1:
time: 547 us; the launch traced here: 546 us
  waiting for transfers between devices  300 us (55%)
  Pallas kernels  98.9 us (18%)
  matrix products  52.7 us (10%)
  blocking collectives  33 us (6%)
  local copies, waits for them, and re-layouts  25.1 us (5%)
  starting transfers between devices  15.7 us (3%)
  between operations  14.2 us (3%)
  other arithmetic  7 us (1%)
    all_to_all x4, waiting for transfers between devices, exchange(): lax.all_to_all(a.reshape(n_dev, rows, n_loc, dim), 'sp', 0, 0, tiled=True)  112 us
    psum x1, waiting for transfers between devices, local_step(): d_wq, d_wk, d_wv, d_ng, d_qg, d_kg = lax.psum(late, 'sp')  97.7 us
    psum x1, waiting for transfers between devices, local_step(): d_wo = lax.psum(dot(o, dy_flat, 0, 0), 'sp')  90.2 us
    pallas_call x1, Pallas kernels, attention_bwd(): pl.pallas_call(bwd_kernel, grid=(rows, kv_heads), in_specs=[pl.BlockSpec(...  54.6 us
    dot_general x8, matrix products, dot(): lax.dot_general(a, b, (((ca,), (cb,)), ((), ())), preferred_element_type=...  52.7 us
    pallas_call x1, Pallas kernels, attention_fwd(): pl.pallas_call(fwd_kernel, grid=(rows, kv_heads), in_specs=[pl.BlockSpec(...  44.4 us
    psum x1, blocking collectives, local_step(): d_wq, d_wk, d_wv, d_ng, d_qg, d_kg = lax.psum(late, 'sp')  33 us
    unnamed x48, local copies, waits for them, and re-layouts  25 us
  transfers between devices with their start and end apart: 6, of which 5 were waited for; matrix products, arithmetic and copies ran while one was open for 7% of the time, Pallas kernels for 8%

profile of v1, /device:TPU:0, one launch (start us, length us, event | category | flops | bytes accessed | tf_op | source)
XLA Modules:
  0.0 546.4 jit_solution(5598239776515941091)
XLA Ops:
  7.2 5.3 all-to-all-start
  12.5 27.6 %all-to-all-done.x_ref = bf16[16,2,32,1024]{3,2,1,0:T(8,128)(2,1)S(1)} async-done(((bf16[16,2,32,1024]{3,2,1,0:T(8,128)(2,1)}), bf16[16,2,32,1024]{3,2,1,0:T(8,128)(2,1)S(1)}, u32[]{:S(2)}, u32[]{:S(2)}) %all-to-all-start) | async-done | bytes 2097184 | tf_op jit(solution)/shard_map/all_to_all | solution.py:224
  40.1 0.0 copy-start
  40.1 3.9 all-to-all-start.2
  44.1 0.0 all-reduce.5.cloned.1.call-start
  44.1 1.0 fusion.10
  45.1 1.0 pad_maximum_fusion
  46.1 0.5 fusion.8
  46.6 0.0 copy-done
  46.6 0.1 rsqrt.12
  46.7 44.4 %attn_fwd.1 = (bf16[16,2,32,1024]{3,2,1,0:T(8,128)(2,1)}, bf16[2,512,2048]{2,1,0:T(8,128)(2,1)}, bf16[2,512,1024]{2,1,0:T(8,128)(2,1)}, bf16[2,512,2048]{2,1,0:T...) custom-call(bf16[16,2,32,1024]{3,2,1,0:T(8,128)(2,1)} %copy-done, ...), custom_call_target="tpu_custom_call" | custom-call | flops 12000000000 | bytes 50000000 | tf_op jit(solution)/shard_map/attn_fwd/pallas_call | solution.py:152
  91.1 0.0 all-to-all-done.2.dy_ref
  91.1 0.0 copy-start.13
  91.1 54.6 %attn_bwd.1 = (bf16[16,2,32,2048]{3,2,1,0:T(8,128)(2,1)}, bf16[16,2,32,1024]{3,2,1,0:T(8,128)(2,1)}, bf16[16,2,32,1024]{3,2,1,0:T(8,128)(2,1)}, f32[1,128]{1,0:T(1,128)}, f32[1,128]{1,0:T(1,128)}) custom-call(bf16[16,2,32,1024]{3,2,1,0:T(8,128)(2,1)} %all-to-all-done.2.dy_ref, bf16[2048,1024]{1,0:T(8,128)(2,1)} %wo_ref.1, ...), custom_call_target="tpu_custom_call" | custom-call | flops 14000000000 | bytes 50000000 | tf_op jit(solution)/shard_map/attn_bwd/pallas_call | solution.py:188
  145.7 0.0 copy-done.13
  145.7 0.0 copy-start.12
  145.7 0.0 copy-start.15
  145.7 6.1 %fusion.12 = f32[1024,1024]{1,0:T(8,128)} fusion(bf16[1024,1024]{1,0:T(8,128)(2,1)} %bitcast.88, bf16[1024,1024]{1,0:T(8,128)(2,1)S(1)} %copy-done.13), kind=kOutput, calls=%fused_computation.29 | convolution fusion | flops 2147483648 | bytes 8388608 | tf_op jit(solution)/shard_map/dot_general | solution.py:19
  151.8 0.0 copy-done.12
  151.9 0.0 copy-done.15
  151.9 6.1 %fusion.11 = f32[1024,1024]{1,0:T(8,128)} fusion(bf16[1024,2048]{1,0:T(8,128)(2,1)S(1)} %bitcast.87, bf16[1024,2048]{1,0:T(8,128)(2,1)S(1)} %copy-done.12), kind=kOutput, calls=%fused_computation.28 | convolution fusion | flops 4294967296 | bytes 12582912 | tf_op jit(solution)/shard_map/dot_general | solution.py:19
  157.9 0.0 copy-done.14
  157.9 8.5 %convolution_bitcast_fusion = f32[2048,1024]{1,0:T(8,128)} fusion(bf16[16,2,32,2048]{3,2,1,0:T(8,128)(2,1)S(1)} %copy-done.14, bf16[16,2,32,1024]{3,2,1,0:T(8,128)(2,1)} %all-to-all-done.2.dy_ref), kind=kOutput, calls=%fused_computation | convolution fusion | flops 4294967296 | bytes 14680064 | tf_op jit(solution)/shard_map/dot_general | solution.py:19
  166.4 0.0 all-reduce.5.cloned.1.call-update
  166.4 0.2 all-reduce.7.cloned.1.call-start
  166.7 1.3 copy-done.17
  168.0 6.1 %convolution_bitcast_fusion.3 = f32[1024,1024]{1,0:T(8,128)} fusion(bf16[16,2,32,1024]{3,2,1,0:T(8,128)(2,1)} %get-tuple-element.39, bf16[16,2,32,1024]{3,2,1,0:T(8,128)(2,1)S(1)} %copy-done.17), kind=kOutput, calls=%fused_computation.18 | convolution fusion | flops 2147483648 | bytes 8388608 | tf_op jit(solution)/shard_map/dot_general | solution.py:19
  174.1 0.0 copy-done.8
  174.1 0.0 copy-done.18
  174.1 0.0 copy-start.6
  174.1 0.0 copy-start.7
  174.1 0.0 copy-start.9
  174.1 4.6 convolution_bitcast_fusion.2
  178.7 0.0 copy-done.1
  178.7 0.0 copy-done.5
  178.7 0.8 copy-done.6
  179.5 0.8 copy-done.7
  180.2 0.0 copy-done.9
  180.2 5.3 fusion.7
  185.5 0.0 copy-done.16
  185.5 6.9 %convolution_bitcast_fusion.1 = f32[1024,2048]{1,0:T(8,128)} fusion(bf16[16,2,32,1024]{3,2,1,0:T(8,128)(2,1)S(1)} %copy-done.18, bf16[16,2,32,2048]{3,2,1,0:T(8,128)(2,1)S(1)} %copy-done.16), kind=kOutput, calls=%fused_computation.1 | convolution fusion | flops 4294967296 | bytes 14680064 | tf_op jit(solution)/shard_map/dot_general | solution.py:19
  192.4 90.2 %all-reduce.5.cloned.1.call-done = f32[2048,1024]{1,0:T(8,128)} async-done(((f32[2048,1024]{1,0:T(8,128)}), f32[2048,1024]{1,0:T(8,128)}) %all-reduce.5.cloned.1.call-update) | async-done | bytes 8388624 | tf_op jit(solution)/shard_map/psum | solution.py:233
  282.6 0.0 all-reduce.7.cloned.1.call-update
  282.6 9.3 %fusion.9 = bf16[1024,1024]{1,0:T(8,128)(2,1)} fusion(bf16[16,2,32,1024]{3,2,1,0:T(8,128)(2,1)S(1)} %copy-done.1, bf16[1024,2048]{1,0:T(8,128)(2,1)} %bitcast.86, bf16[2048,1024]{1,0:T(8,128)(2,1)} %wo_ref.1), kind=kOutput, calls=%fused_computation.15 | convolution fusion | flops 4298113024 | bytes 12582912 | tf_op jit(solution)/shard_map/dot_general | solution.py:19
  291.9 3.2 all-to-all-start.1
  295.1 4.5 fusion
  299.5 41.5 %all-to-all-done.1 = bf16[16,2,32,1024]{3,2,1,0:T(8,128)(2,1)} async-done(((bf16[16,2,32,1024]{3,2,1,0:T(8,128)(2,1)}), bf16[16,2,32,1024]{3,2,1,0:T(8,128)(2,1)}, u32[]{:S(2)}, u32[]{:S(2)}) %all-to-all-start.1) | async-done | bytes 2097184 | tf_op jit(solution)/shard_map/all_to_all | solution.py:224
  341.1 3.0 all-to-all-start.3
  344.1 42.7 %all-to-all-done.3 = bf16[16,2,32,1024]{3,2,1,0:T(8,128)(2,1)S(1)} async-done(((bf16[16,2,32,1024]{3,2,1,0:T(8,128)(2,1)}), bf16[16,2,32,1024]{3,2,1,0:T(8,128)(2,1)S(1)}, u32[]{:S(2)}, u32[]{:S(2)}) %all-to-all-start.3) | async-done | bytes 2097184 | tf_op jit(solution)/shard_map/all_to_all | solution.py:224
  386.8 0.0 copy-done.10
  386.8 0.0 copy-done.11
  386.8 33.0 %all-reduce = (f32[1024]{0:T(1024)}, f32[128]{0:T(128)}, f32[128]{0:T(128)}) all-reduce(f32[1024]{0:T(1024)S(1)} %get-tuple-element.46, f32[128]{0:T(128)S(1)} %bitcast.80, f32[128]{0:T(128)S(1)} %bitcast.81), channel_id=1, replica_groups=mesh['sp'=16] {'sp'}, use_global_device_ids=true, to_apply=%region_7.0 | all-reduce | flops 1280 | bytes 10240 | tf_op jit(solution)/shard_map/psum | solution.py:251
  419.8 97.7 %all-reduce.7.cloned.1.call-done = (f32[1024,2048]{1,0:T(8,128)}, f32[1024,1024]{1,0:T(8,128)}, f32[1024,1024]{1,0:T(8,128)}) async-done(((f32[1024,2048]{1,0:T(8,128)}, f32[1024,1024]{1,0:T(8,128)}, f32[1024,1024]{1,0:T(8,128)}), (f32[1024,2048]{1,0:T(8,128)}, f32[1024,1024]{1,0:T(8,128)}, f32[1024,1024]{1,0:T(8,128)})) %all-reduce.7.cloned.1.call-update) | async-done | bytes 16777232 | tf_op jit(solution)/shard_map/psum | solution.py:251
  517.5 3.3 copy.28
  520.9 1.3 copy.29
  522.2 0.9 copy-done.2
  523.1 4.3 copy.30
  527.3 1.0 copy-done.4
  528.3 2.1 copy.31
  530.4 1.6 copy-done.3
  532.0 2.1 copy.32
  534.1 0.0 slice-done
  534.1 2.1 slice-done.1
  536.2 3.4 copy.33
  (19 shorter events, 0.1 us)
Async XLA Ops:
  7.2 32.9 %all-to-all-start = ((bf16[16,2,32,1024]{3,2,1,0:T(8,128)(2,1)}), bf16[16,2,32,1024]{3,2,1,0:T(8,128)(2,1)S(1)}, u32[]{:S(2)}, u32[]{:S(2)}) async-start(bf16[16,2,32,1024]{3,2,1,0:T(8,128)(2,1)} %bitcast.75), calls=%async_computation | async-start | bytes 4194304 | tf_op jit(solution)/shard_map/all_to_all | solution.py:224
  40.1 6.5 %copy-start = (bf16[16,2,32,1024]{3,2,1,0:T(8,128)(2,1)}, bf16[16,2,32,1024]{3,2,1,0:T(8,128)(2,1)S(1)}, u32[]{:S(2)}) copy-start(bf16[16,2,32,1024]{3,2,1,0:T(8,128)(2,1)S(1)} %all-to-all-done.x_ref) | copy-start | bytes 6291460
  40.1 51.0 %all-to-all-start.2 = ((bf16[16,2,32,1024]{3,2,1,0:T(8,128)(2,1)}), bf16[16,2,32,1024]{3,2,1,0:T(8,128)(2,1)}, u32[]{:S(2)}, u32[]{:S(2)}) async-start(bf16[16,2,32,1024]{3,2,1,0:T(8,128)(2,1)} %bitcast.76), calls=%async_computation.2 | async-start | bytes 4194304 | tf_op jit(solution)/shard_map/all_to_all | solution.py:224
  44.1 238.5 %all-reduce.5.cloned.1.call-start = ((), (), s32[]{:S(2)}) async-start(), calls=%async_computation.4 | async-start | bytes 16777216 | tf_op jit(solution)/shard_map/psum | solution.py:233
  91.1 54.6 %copy-start.13 = (bf16[1024,1024]{1,0:T(8,128)(2,1)S(1)}, bf16[1024,1024]{1,0:T(8,128)(2,1)}, u32[]{:S(2)}) copy-start(bf16[1024,1024]{1,0:T(8,128)(2,1)} %wk_ref.1) | copy-start | bytes 6291460
  145.7 6.2 %copy-start.12 = (bf16[1024,2048]{1,0:T(8,128)(2,1)S(1)}, bf16[1024,2048]{1,0:T(8,128)(2,1)}, u32[]{:S(2)}) copy-start(bf16[1024,2048]{1,0:T(8,128)(2,1)} %wq_ref.1) | copy-start | bytes 12582916
  145.7 6.1 %copy-start.15 = (bf16[16,2,32,2048]{3,2,1,0:T(8,128)(2,1)S(1)}, bf16[16,2,32,2048]{3,2,1,0:T(8,128)(2,1)}, u32[]{:S(2)}) copy-start(bf16[16,2,32,2048]{3,2,1,0:T(8,128)(2,1)} %get-tuple-element.36) | copy-start | bytes 12582916
  151.9 6.1 %copy-start.14 = (bf16[16,2,32,2048]{3,2,1,0:T(8,128)(2,1)S(1)}, bf16[16,2,32,2048]{3,2,1,0:T(8,128)(2,1)}, u32[]{:S(2)}) copy-start(bf16[16,2,32,2048]{3,2,1,0:T(8,128)(2,1)} %get-tuple-element.29) | copy-start | bytes 12582916
  166.4 1.6 copy-start.17
  166.4 351.1 %all-reduce.7.cloned.1.call-start = ((), (), s32[]{:S(2)}) async-start(), calls=%async_computation.5 | async-start | bytes 33554432 | tf_op jit(solution)/shard_map/psum | solution.py:251
  168.0 6.1 %copy-start.8 = (bf16[16,2,32,1024]{3,2,1,0:T(8,128)(2,1)S(1)}, bf16[16,2,32,1024]{3,2,1,0:T(8,128)(2,1)}, u32[]{:S(2)}) copy-start(bf16[16,2,32,1024]{3,2,1,0:T(8,128)(2,1)} %get-tuple-element.38) | copy-start | bytes 6291460
  168.0 6.1 %copy-start.18 = (bf16[16,2,32,1024]{3,2,1,0:T(8,128)(2,1)S(1)}, bf16[16,2,32,1024]{3,2,1,0:T(8,128)(2,1)}, u32[]{:S(2)}) copy-start(bf16[16,2,32,1024]{3,2,1,0:T(8,128)(2,1)} %get-tuple-element.39) | copy-start | bytes 6291460
  174.1 4.6 copy-start.1
  174.1 4.6 copy-start.5
  174.1 5.4 copy-start.6
  174.1 6.1 %copy-start.7 = (bf16[1024,1024]{1,0:T(8,128)(2,1)S(1)}, bf16[1024,1024]{1,0:T(8,128)(2,1)}, u32[]{:S(2)}) copy-start(bf16[1024,1024]{1,0:T(8,128)(2,1)} %wv_ref.1) | copy-start | bytes 6291460
  174.1 6.1 %copy-start.9 = (f32[1024]{0:T(1024)S(1)}, f32[1024]{0:T(1024)}, u32[]{:S(2)}) copy-start(f32[1024]{0:T(1024)} %param.10) | copy-start | bytes 12292
  180.2 5.3 copy-start.16
  291.9 49.2 %all-to-all-start.1 = ((bf16[16,2,32,1024]{3,2,1,0:T(8,128)(2,1)}), bf16[16,2,32,1024]{3,2,1,0:T(8,128)(2,1)}, u32[]{:S(2)}, u32[]{:S(2)}) async-start(bf16[16,2,32,1024]{3,2,1,0:T(8,128)(2,1)} %bitcast.77), calls=%async_computation.1 | async-start | bytes 4194304 | tf_op jit(solution)/shard_map/all_to_all | solution.py:224
  299.5 87.3 %copy-start.10 = (f32[1,128]{1,0:T(1,128)S(1)}, f32[1,128]{1,0:T(1,128)}, u32[]{:S(2)}) copy-start(f32[1,128]{1,0:T(1,128)} %get-tuple-element.40) | copy-start | bytes 1540
  299.5 87.3 %copy-start.11 = (f32[1,128]{1,0:T(1,128)S(1)}, f32[1,128]{1,0:T(1,128)}, u32[]{:S(2)}) copy-start(f32[1,128]{1,0:T(1,128)} %get-tuple-element.41) | copy-start | bytes 1540
  341.1 45.8 %all-to-all-start.3 = ((bf16[16,2,32,1024]{3,2,1,0:T(8,128)(2,1)}), bf16[16,2,32,1024]{3,2,1,0:T(8,128)(2,1)S(1)}, u32[]{:S(2)}, u32[]{:S(2)}) async-start(bf16[16,2,32,1024]{3,2,1,0:T(8,128)(2,1)} %bitcast.74), calls=%async_computation.3 | async-start | bytes 4194304 | tf_op jit(solution)/shard_map/all_to_all | solution.py:224
  517.5 5.5 %copy-start.2 = (f32[1024,2048]{1,0:T(8,128)S(1)}, f32[1024,2048]{1,0:T(8,128)}, u32[]{:S(2)}) copy-start(f32[1024,2048]{1,0:T(8,128)} %get-tuple-element.74) | copy-start | bytes 25165828
  523.1 5.2 copy-start.4
  528.3 3.7 copy-start.3
  528.3 5.8 %slice-start = ((s8[8388608]{0:T(1024)(128)(4,1)}), s8[4194304]{0:T(1024)(128)(4,1)S(1)}, s32[]{:S(2)}) async-start(s8[8388608]{0:T(1024)(128)(4,1)} %bitcast.71), calls=%async_computation.6 | async-start | bytes 8388608
  532.0 4.2 slice-start.1
Sparse Core Ops, SparseCore 0:
  166.5 115.9 all-reduce.4
  289.4 228.0 all-reduce.6

commit v2 on v0

v2 whole, which is shorter than its diff:
```python
import math
import jax
import jax.numpy as jnp
import numpy as np
from jax import lax
from jax.experimental import pallas as pl
from jax.experimental.pallas import tpu as pltpu
from jax.sharding import PartitionSpec as P

ROPE_BASE = 1000000.0
NORM_EPS = 1e-6
LOG2E = 1.4426950408889634
F32 = jnp.float32
BF16 = jnp.bfloat16
QBLK = 256
VMEM_LIMIT = 67043328
COLOURS = ((1, 2, 3), (2, 3, 1), (3, 1, 2))


def dot(a, b, ca, cb):
    return lax.dot_general(a, b, (((ca,), (cb,)), ((), ())), preferred_element_type=F32)


def rope_tables(n_pos, head_dim):
    half_dim = head_dim // 2
    inv_freq = np.exp(np.arange(half_dim, dtype=np.float32) * np.float32(-2.0 * math.log(ROPE_BASE) / head_dim))
    angles = np.arange(n_pos, dtype=np.float32)[:, None] * inv_freq[None, :]
    cos, sin = np.cos(angles), np.sin(angles)
    return np.concatenate([cos, cos], axis=-1), np.concatenate([-sin, sin], axis=-1)


def norm_rope(raw, gain, cos, sin):
    inv = lax.rsqrt(jnp.mean(raw * raw, axis=-1, keepdims=True) + NORM_EPS)
    unit = raw * inv
    normed = unit * gain
    return normed * cos + pltpu.roll(normed, raw.shape[-1] // 2, 1) * sin, unit, inv


def norm_rope_back(d_rot, unit, inv, gain, cos, sin):
    d_normed = d_rot * cos - pltpu.roll(d_rot, unit.shape[-1] // 2, 1) * sin
    d_gain = jnp.sum(d_normed * unit, axis=0, keepdims=True)
    d_unit = d_normed * gain
    return inv * (d_unit - unit * jnp.mean(d_unit * unit, axis=-1, keepdims=True)), d_gain


def causal_mask_t(scores_t, first_q):
    n_q = scores_t.shape[1]
    key = lax.broadcasted_iota(jnp.int32, (n_q, n_q), 0)
    query = lax.broadcasted_iota(jnp.int32, (n_q, n_q), 1)
    diag = jnp.where(query >= key, scores_t[first_q:], -1e30)
    if first_q == 0:
        return diag
    return jnp.concatenate([scores_t[:first_q], diag], axis=0)


def block_kernel(n_groups, hid_ref, dyin_ref, gain_ref, wq_ref, wk_ref, wv_ref, wo_ref, qg_ref, kg_ref, cos_ref, sin_ref,
                 y_ref, dx_ref, dwq_ref, dwk_ref, dwv_ref, dwo_ref, small_ref,
                 xs, dys, hs, ht, wcat, dqkv, oall, y_acc, dn_acc, u, r0, r1, r2, r3, r4, sm, smr,
                 in_send, in_recv, in_loc, d_send, d_recv, p_send, p_recv, g_send, g_recv, e_send, e_recv,
                 s_send, s_recv, o_sem, out_send, out_recv, out_loc):
    n_dev, rows, n_loc, dim = hid_ref.shape
    n_pos = n_dev * n_loc
    head_dim = qg_ref.shape[-1]
    qw = wq_ref.shape[1]
    group = qw // head_dim
    width = qw + 2 * head_dim
    half = u.shape[1] // 2
    blk = half // 3
    step = pl.program_id(0)
    me = lax.axis_index('sp')
    bit = [(me // (1 << i)) % 2 for i in range(4)]
    partner = [me + (1 << i) * (1 - 2 * bit[i]) for i in range(4)]

    def remote(src, dst, send, recv, device):
        return pltpu.make_async_remote_copy(src_ref=src, dst_ref=dst, send_sem=send, recv_sem=recv,
                                            device_id=(device,), device_id_type=pl.DeviceIdType.MESH)

    def rows_of(g, start, size):
        return u.at[g, pl.ds(pl.multiple_of(start, 32), size)]

    own, other = bit[0] * half, (1 - bit[0]) * half
    keep1, send1, keep2, send2, keep3, send3 = [], [], [], [], [], []
    for c, (d1, d2, d3) in enumerate(COLOURS):
        base = own + c * blk
        keep1.append(base + bit[d1] * (blk // 2))
        send1.append(base + (1 - bit[d1]) * (blk // 2))
        keep2.append(keep1[c] + bit[d2] * (blk // 4))
        send2.append(keep1[c] + (1 - bit[d2]) * (blk // 4))
        keep3.append(keep2[c] + bit[d3] * (blk // 8))
        send3.append(keep2[c] + (1 - bit[d3]) * (blk // 8))

    def core_scatter(g):
        return remote(rows_of(g, other, half), r0.at[g % 2], d_send.at[g % 2], d_recv.at[g % 2], partner[0])

    def scatter(phase, c, g):
        start, size, buf = ((send1, blk // 2, r1), (send2, blk // 4, r2), (send3, blk // 8, r3))[phase]
        return remote(rows_of(g, start[c], size), buf.at[g % 2, c], p_send.at[phase, c, g % 2], p_recv.at[phase, c, g % 2],
                      partner[COLOURS[c][phase]])

    def gather(phase, c, g):
        start, size = ((keep3, blk // 8), (keep2, blk // 4), (keep1, blk // 2))[phase]
        part = rows_of(g, start[c], size)
        return remote(part, part if phase else r4.at[g % 2, c], g_send.at[phase, c, g % 2], g_recv.at[phase, c, g % 2], partner[COLOURS[c][2 - phase]])

    def core_gather(g):
        part = rows_of(g, own, half)
        return remote(part, part, e_send.at[g % 2], e_recv.at[g % 2], partner[0])

    def out_copies(g):
        part = u.at[g]
        col = lambda n: pl.ds(pl.multiple_of(g * n, 128), n)
        orow = pl.ds(pl.multiple_of(g * qw, 128), qw)
        pieces = ((part.at[:dim, :qw], dwq_ref.at[:, col(qw)]),
                  (part.at[:dim, qw:qw + head_dim], dwk_ref.at[:, col(head_dim)]),
                  (part.at[:dim, qw + head_dim:], dwv_ref.at[:, col(head_dim)]),
                  (part.at[dim:dim + qw], dwo_ref.at[orow, :width]),
                  (part.at[dim + qw:], dwo_ref.at[orow, width:]))
        return [pltpu.make_async_copy(a, b, o_sem.at[i]) for i, (a, b) in enumerate(pieces)]

    def add_rows(g, start, size, buf):
        s = pl.ds(pl.multiple_of(start, 32), size)
        u[g, s] = u[g, s] + buf

    def stage(k, g):
        slot = g % 2
        if k == 1:
            core_scatter(g).wait()
            for c in range(3):
                add_rows(g, own + c * blk, blk, r0[slot, c * blk:(c + 1) * blk])
                scatter(0, c, g).start()
        elif k in (2, 3, 4):
            keep, size, buf = ((keep1, blk // 2, r1), (keep2, blk // 4, r2), (keep3, blk // 8, r3))[k - 2]
            for c in range(3):
                scatter(k - 2, c, g).wait()
            for c in range(3):
                add_rows(g, keep[c], size, buf[slot, c])
                (scatter(k - 1, c, g) if k < 4 else gather(0, c, g)).start()
        elif k in (5, 6):
            for c in range(3):
                gather(k - 5, c, g).wait()
            for c in range(3):
                if k == 5:
                    u[g, pl.ds(pl.multiple_of(send3[c], 32), blk // 8)] = r4[slot, c]
                gather(k - 4, c, g).start()
        elif k == 7:
            for c in range(3):
                gather(2, c, g).wait()
            core_gather(g).start()
        else:
            core_gather(g).wait()

            @pl.when(g > 0)
            def _():
                for copy in out_copies(g - 1):
                    copy.wait()
            for copy in out_copies(g):
                copy.start()

    def handler(sub):
        for k in range(8, 0, -1):
            if (sub - 2 - k) % 3 == 0:
                g = step + (sub - 2 - k) // 3

                @pl.when((g >= 0) & (g < n_groups))
                def _():
                    stage(k, g)
        for i in range(5):
            if i % 3 == sub:
                @pl.when(step == n_groups + i // 3)
                def _():
                    if i == 0:
                        small_copy(0).start()
                    else:
                        small_step(i - 1)

    def small_copy(i):
        return remote(sm.at[i], smr.at[i], s_send.at[i], s_recv.at[i], partner[i])

    def small_step(i):
        small_copy(i).wait()
        sm[i + 1] = sm[i] + smr[i]
        if i < 3:
            small_copy(i + 1).start()
        else:
            small_ref[...] = sm[4]

    def in_copy(which, row, peer):
        src, dst = (hid_ref, xs) if which == 0 else (dyin_ref, dys)
        n = 2 * row + which
        return remote(src.at[peer, row], dst.at[row, me], in_send.at[n], in_recv.at[n], peer)

    def in_local(which, row):
        src, dst = (hid_ref, xs) if which == 0 else (dyin_ref, dys)
        return pltpu.make_async_copy(src.at[me, row], dst.at[row, me], in_loc.at[2 * row + which])

    def in_wait(which, row):
        dst = xs if which == 0 else dys
        n = 2 * row + which
        many = dst.at[row, pl.ds(0, n_dev - 1)]
        pltpu.make_async_copy(many, many, in_recv.at[n]).wait()
        in_local(which, row).wait()

    def in_wait_send(which, row):
        many = (xs if which == 0 else dys).at[row, pl.ds(0, n_dev - 1)]
        pltpu.make_async_copy(many, many, in_send.at[2 * row + which]).wait()

    def out_copy(which, row, peer):
        src, dst = (xs, y_ref) if which == 0 else (dys, dx_ref)
        n = 2 * row + which
        return remote(src.at[row, peer], dst.at[me, row], out_send.at[n], out_recv.at[n], peer)

    def out_local(which, row):
        src, dst = (xs, y_ref) if which == 0 else (dys, dx_ref)
        return pltpu.make_async_copy(src.at[row, me], dst.at[me, row], out_loc.at[2 * row + which])

    def to_peers(make, which, row):
        def body(d, carry):
            make(which, row, lax.rem(me + d, n_dev)).start()
            return carry
        lax.fori_loop(1, n_dev, body, 0)

    @pl.when(step == 0)
    def _():
        barrier = pltpu.get_barrier_semaphore()

        def greet(d, carry):
            pl.semaphore_signal(barrier, inc=1, device_id=(lax.rem(me + d, n_dev),), device_id_type=pl.DeviceIdType.MESH)
            return carry
        lax.fori_loop(1, n_dev, greet, 0)
        pl.semaphore_wait(barrier, n_dev - 1)
        for row in range(rows):
            for which in range(2):
                in_local(which, row).start()
                to_peers(in_copy, which, row)
        y_acc[...] = jnp.zeros_like(y_acc)
        dn_acc[...] = jnp.zeros_like(dn_acc)
        sm[0] = jnp.zeros_like(sm[0])

    def tokens_of(row):
        return slice(row * n_pos, (row + 1) * n_pos)

    def row_compute(row):
        tok = tokens_of(row)
        cos, sin = cos_ref[...], sin_ref[...]
        scale = head_dim ** -0.5
        qkv = dot(hs[tok], wcat[...], 1, 0).astype(BF16)
        d_o = dot(dys[row].reshape(n_pos, dim), wo_ref[...], 1, 1).astype(BF16)
        k_rot, k_unit, k_inv = norm_rope(qkv[:, qw:qw + head_dim].astype(F32), kg_ref[...], cos, sin)
        k_rot = k_rot.astype(BF16)
        v = qkv[:, qw + head_dim:]
        dk_sum = [jnp.zeros((QBLK, head_dim), F32) for _ in range(n_pos // QBLK)]
        dv_sum = [jnp.zeros((QBLK, head_dim), F32) for _ in range(n_pos // QBLK)]
        for j in range(group):
            cols = slice(j * head_dim, (j + 1) * head_dim)
            q_rot, q_unit, q_inv = norm_rope(qkv[:, cols].astype(F32), qg_ref[...], cos, sin)
            q_rot = q_rot.astype(BF16)
            dq_parts = []
            for first in range(0, n_pos, QBLK):
                n_key = first + QBLK
                q_blk = q_rot[first:n_key]
                do_blk = d_o[first:n_key, cols]
                scores = causal_mask_t(dot(k_rot[:n_key], q_blk, 1, 1) * (scale * LOG2E), first)
                e = jnp.exp2(scores - jnp.max(scores, axis=0, keepdims=True))
                prob = e * (1.0 / jnp.sum(e, axis=0, keepdims=True))
                prob_bf = prob.astype(BF16)
                oall[row * n_pos + first:row * n_pos + n_key, cols] = dot(prob_bf, v[:n_key], 0, 0).astype(BF16)
                d_prob = dot(v[:n_key], do_blk, 1, 1)
                inner = jnp.sum(prob * d_prob, axis=0, keepdims=True)
                d_scores = (prob * (d_prob - inner) * scale).astype(BF16)
                dv_blk = dot(prob_bf, do_blk, 1, 0)
                dk_blk = dot(d_scores, q_blk, 1, 0)
                for i in range(n_key // QBLK):
                    dv_sum[i] += dv_blk[i * QBLK:(i + 1) * QBLK]
                    dk_sum[i] += dk_blk[i * QBLK:(i + 1) * QBLK]
                dq_parts.append(dot(d_scores, k_rot[:n_key], 0, 0))
            dq = jnp.concatenate(dq_parts, axis=0).astype(BF16).astype(F32)
            dq_raw, d_gain = norm_rope_back(dq, q_unit, q_inv, qg_ref[...], cos, sin)
            dqkv[tok, cols] = dq_raw.astype(BF16)
            sm[0, 1:2, :head_dim] += d_gain
        dk = jnp.concatenate(dk_sum, axis=0).astype(BF16).astype(F32)
        dk_raw, d_gain = norm_rope_back(dk, k_unit, k_inv, kg_ref[...], cos, sin)
        dqkv[tok, qw:qw + head_dim] = dk_raw.astype(BF16)
        sm[0, 1:2, head_dim:2 * head_dim] += d_gain
        dqkv[tok, qw + head_dim:] = jnp.concatenate(dv_sum, axis=0).astype(BF16)

    def input_norm(row):
        x = xs[row].reshape(n_pos, dim).astype(F32)
        inv = lax.rsqrt(jnp.mean(x * x, axis=-1, keepdims=True) + NORM_EPS)
        h = (x * inv * gain_ref[...]).astype(BF16)
        hs[tokens_of(row)] = h
        ht[:, tokens_of(row)] = h.T

    def finish_row(row):
        tok = tokens_of(row)
        x = xs[row].reshape(n_pos, dim).astype(F32)
        inv = lax.rsqrt(jnp.mean(x * x, axis=-1, keepdims=True) + NORM_EPS)
        unit = x * inv
        d_normed = dn_acc[tok]
        sm[0, 0:1] += jnp.sum(d_normed * unit, axis=0, keepdims=True)
        d_unit = d_normed * gain_ref[...]
        d_x = inv * (d_unit - unit * jnp.mean(d_unit * unit, axis=-1, keepdims=True))
        d_y = dys[row].reshape(n_pos, dim).astype(F32)
        dys[row] = (d_y + d_x).astype(BF16).reshape(n_dev, n_loc, dim)
        xs[row] = (x + y_acc[tok]).astype(BF16).reshape(n_dev, n_loc, dim)

    computing = step < n_groups

    @pl.when(computing)
    def _():
        wcat[:, :qw] = wq_ref[...]
        wcat[:, qw:qw + head_dim] = wk_ref[...]
        wcat[:, qw + head_dim:] = wv_ref[...]

    for row in range(rows):
        handler(row)

        @pl.when(step == 0)
        def _():
            in_wait(0, row)
            input_norm(row)
            in_wait(1, row)

        @pl.when(computing)
        def _():
            row_compute(row)

    handler(2)

    @pl.when(computing)
    def _():
        u[step, :dim] = dot(ht[...], dqkv[...], 1, 0)
        d_wo = dot(oall[...], dys[...].reshape(rows * n_pos, dim), 0, 0)
        u[step, dim:dim + qw] = d_wo[:, :width]
        u[step, dim + qw:] = d_wo[:, width:]
        core_scatter(step).start()
        y_acc[...] += dot(oall[...], wo_ref[...], 1, 0)
        dn_acc[...] += dot(dqkv[...], wcat[...], 1, 1)

    @pl.when(step == n_groups - 1)
    def _():
        for row in range(rows):
            for which in range(2):
                in_wait_send(which, row)
        for row in range(rows):
            finish_row(row)
            for which in (1, 0):
                out_local(which, row).start()
                to_peers(out_copy, which, row)

    @pl.when(step == pl.num_programs(0) - 1)
    def _():
        for copy in out_copies(n_groups - 1):
            copy.wait()
        for row in range(rows):
            for which in range(2):
                n = 2 * row + which
                many = (xs if which == 0 else dys).at[row, pl.ds(0, n_dev - 1)]
                landed = (y_ref if which == 0 else dx_ref).at[pl.ds(0, n_dev - 1), row]
                pltpu.make_async_copy(many, many, out_send.at[n]).wait()
                pltpu.make_async_copy(landed, landed, out_recv.at[n]).wait()
                out_local(which, row).wait()


def solution(mesh):
    n_dev = mesh.shape['sp']
    seq_spec = P(None, 'sp', None)
    replicated = P()

    def local_step(hidden, norm_gain, w_q, w_k, w_v, q_gain, k_gain, w_o, d_out):
        n_batch, n_loc, dim = hidden.shape
        head_dim = q_gain.shape[0]
        kv_heads = w_k.shape[1] // head_dim
        qw = w_q.shape[1] // kv_heads
        width = qw + 2 * head_dim
        rows = n_batch // n_dev
        n_pos = n_loc * n_dev
        tokens = rows * n_pos
        cos, sin = rope_tables(n_pos, head_dim)
        slice_rows = dim + 2 * qw
        blk = slice_rows // 6
        last = lambda t: jnp.minimum(t, kv_heads - 1)
        const = lambda shape: pl.BlockSpec(shape, lambda t: (0, 0))
        anywhere = pl.BlockSpec(memory_space=pl.ANY)
        act = (n_dev, rows, n_loc, dim)
        dma = pltpu.SemaphoreType.DMA
        y, d_hidden, d_wq, d_wk, d_wv, d_wo, small = pl.pallas_call(
            lambda *refs: block_kernel(kv_heads, *refs),
            grid=(kv_heads + 3,),
            in_specs=[
                anywhere, anywhere, const((1, dim)),
                pl.BlockSpec((dim, qw), lambda t: (0, last(t))),
                pl.BlockSpec((dim, head_dim), lambda t: (0, last(t))),
                pl.BlockSpec((dim, head_dim), lambda t: (0, last(t))),
                pl.BlockSpec((qw, dim), lambda t: (last(t), 0)),
                const((1, head_dim)), const((1, head_dim)), const((n_pos, head_dim)), const((n_pos, head_dim))],
            out_specs=[anywhere] * 6 + [const((8, dim))],
            out_shape=[
                jax.ShapeDtypeStruct(act, BF16), jax.ShapeDtypeStruct(act, BF16),
                jax.ShapeDtypeStruct(w_q.shape, F32), jax.ShapeDtypeStruct(w_k.shape, F32),
                jax.ShapeDtypeStruct(w_v.shape, F32), jax.ShapeDtypeStruct(w_o.shape, F32),
                jax.ShapeDtypeStruct((8, dim), F32)],
            scratch_shapes=[
                pltpu.VMEM((rows, n_dev, n_loc, dim), BF16), pltpu.VMEM((rows, n_dev, n_loc, dim), BF16),
                pltpu.VMEM((tokens, dim), BF16), pltpu.VMEM((dim, tokens), BF16),
                pltpu.VMEM((dim, width), BF16), pltpu.VMEM((tokens, width), BF16), pltpu.VMEM((tokens, qw), BF16),
                pltpu.VMEM((tokens, dim), F32), pltpu.VMEM((tokens, dim), F32),
                pltpu.VMEM((kv_heads, slice_rows, width), F32),
                pltpu.VMEM((2, slice_rows // 2, width), F32), pltpu.VMEM((2, 3, blk // 2, width), F32),
                pltpu.VMEM((2, 3, blk // 4, width), F32), pltpu.VMEM((2, 3, blk // 8, width), F32),
                pltpu.VMEM((2, 3, blk // 8, width), F32),
                pltpu.VMEM((5, 8, dim), F32), pltpu.VMEM((4, 8, dim), F32),
                dma((4,)), dma((4,)), dma((4,)), dma((2,)), dma((2,)), dma((3, 3, 2)), dma((3, 3, 2)),
                dma((3, 3, 2)), dma((3, 3, 2)), dma((2,)), dma((2,)), dma((4,)), dma((4,)), dma((5,)),
                dma((4,)), dma((4,)), dma((4,))],
            compiler_params=pltpu.CompilerParams(
                dimension_semantics=('arbitrary',), vmem_limit_bytes=VMEM_LIMIT, collective_id=0, has_side_effects=True),
            cost_estimate=pl.CostEstimate(flops=52 * 10**9, bytes_accessed=50 * 10**6, transcendentals=0),
            name='attn_block',
        )(hidden.reshape(act), d_out.reshape(act), norm_gain[None], w_q, w_k, w_v, w_o, q_gain[None], k_gain[None],
          jnp.asarray(cos), jnp.asarray(sin))
        return (y.reshape(hidden.shape), d_hidden.reshape(hidden.shape), d_wq, d_wk, d_wv, d_wo,
                small[0], small[1, :head_dim], small[1, head_dim:2 * head_dim])

    return jax.shard_map(local_step, mesh=mesh, in_specs=(seq_spec, replicated, replicated, replicated, replicated, replicated, replicated, replicated, seq_spec), out_specs=(seq_spec, seq_spec, replicated, replicated, replicated, replicated, replicated, replicated, replicated), check_vma=False)
```

time: 904 us -> 324 us (0.36); the launches traced: 894 us -> 324 us
  waiting for transfers between devices: 366 us -> 0 us
  Pallas kernels: 0 us -> 297 us
  matrix products: 175 us -> 0 us
  other arithmetic: 128 us -> 0.01 us
  local copies, waits for them, and re-layouts: 137 us -> 26 us
  starting transfers between devices: 38.2 us -> 0 us
  blocking collectives: 34.5 us -> 0 us
  between operations: 15.1 us -> 0.66 us
    pallas_call x0 -> x1, Pallas kernels: none -> 297 us  [local_step(): pl.pallas_call(lambda *refs: block_kernel(kv_heads, *refs), grid=(kv_head...]
    psum x1 -> x0, waiting for transfers between devices: 189 us -> none  [local_step(): lax.psum(d_wq, 'sp')]
    all_to_all x8 -> x0, waiting for transfers between devices: 177 us -> none  [the longest x1 43.1 us: local_step(): k_here = lax.all_to_all(k_rep, 'sp', 2, 1, tiled=True)]
    dot_general x18 -> x0, matrix products: 175 us -> none  [the longest x1 26.8 us: core_backward(): jnp.einsum('bqkgd,bskd->bkgqs', d_grouped, v_part, preferred_element_type...]
    reduce_sum x8 -> x0, other arithmetic: 47.7 us -> none  [the longest x2 16.3 us: rms_scale(): values * lax.rsqrt(jnp.mean(values * values, axis=-1, keepdims=True) + NO...]
    all_to_all x9 -> x0, local copies, waits for them, and re-layouts: 45.9 us -> none  [the longest x2 7.77 us: local_step(): lax.all_to_all(o_here, 'sp', 1, 2, tiled=True)]
    all_to_all x8 -> x0, starting transfers between devices: 37.9 us -> none  [the longest x1 5.66 us: local_step(): q_here = lax.all_to_all(q_rot.astype(jnp.bfloat16), 'sp', 2, 1, tiled=True)]
    psum x1 -> x0, blocking collectives: 34.5 us -> none  [local_step(): lax.psum(d_ngain, 'sp')]
  transfers between devices with their start and end apart: 9 -> 0, of which waited for: 9 -> 0; matrix products, arithmetic and copies ran while one was open for 30% -> 0% of each run, Pallas kernels for 0% -> 0%
where the time goes in v2:
time: 324 us
  Pallas kernels  297 us (92%)
  local copies, waits for them, and re-layouts  26 us (8%)
    pallas_call x1, Pallas kernels, local_step(): pl.pallas_call(lambda *refs: block_kernel(kv_heads, *refs), grid=(kv_head...  297 us
    unnamed x16, local copies, waits for them, and re-layouts  23.5 us

profile of v2, /device:TPU:0, one launch (start us, length us, event | category | flops | bytes accessed | tf_op | source)
XLA Modules:
  0.0 323.8 jit_solution(11155108011478901166)
XLA Ops:
  0.6 297.1 %attn_block.1 = (bf16[16,2,32,1024]{3,2,1,0:T(8,128)(2,1)}, bf16[16,2,32,1024]{3,2,1,0:T(8,128)(2,1)}, f32[1024,2048]{1,0:T(8,128)}, f32[1024,1024]{1,0:T(8,128)...) custom-call(bf16[16,2,32,1024]{3,2,1,0:T(8,128)(2,1)} %bitcast.17, ...), custom_call_target="tpu_custom_call" | custom-call | flops 51999997952 | bytes 50000000 | tf_op jit(solution)/shard_map/attn_block/pallas_call | solution.py:386
  297.7 1.2 slice_bitcast_fusion
  299.0 1.4 slice.9
  300.3 0.0 copy-start
  300.3 3.3 %copy.26 = bf16[32,32,1024]{2,1,0:T(8,128)(2,1)} copy(bf16[32,32,1024]{2,1,0:T(8,128)(2,1)} %bitcast.15) | data formatting | bytes 4194304
  303.6 3.6 %copy.27 = bf16[32,32,1024]{2,1,0:T(8,128)(2,1)} copy(bf16[32,32,1024]{2,1,0:T(8,128)(2,1)} %bitcast.14) | data formatting | bytes 4194304
  307.3 0.0 copy-done
  307.3 0.0 copy-start.2
  307.3 4.3 %copy.28 = f32[1024,2048]{1,0:T(8,128)} copy(f32[1024,2048]{1,0:T(8,128)S(1)} %copy-done) | data formatting | bytes 16777216
  311.5 1.0 copy-done.2
  312.5 0.0 copy-start.1
  312.5 0.0 slice-start
  312.5 2.1 copy.29
  314.6 1.6 copy-done.1
  316.2 0.0 slice-start.1
  316.2 2.1 copy.30
  318.3 0.0 slice-done
  318.3 2.1 slice-done.1
  320.4 3.4 %copy.31 = f32[2048,1024]{1,0:T(8,128)} copy(f32[2048,1024]{1,0:T(8,128)S(1)} %bitcast.13) | data formatting | bytes 16777216
  (1 shorter events, 0.0 us)
Async XLA Ops:
  300.3 7.0 %copy-start = (f32[1024,2048]{1,0:T(8,128)S(1)}, f32[1024,2048]{1,0:T(8,128)}, u32[]{:S(2)}) copy-start(f32[1024,2048]{1,0:T(8,128)} %get-tuple-element.36) | copy-start | bytes 25165828
  307.3 5.2 %copy-start.2 = (f32[1024,1024]{1,0:T(8,128)S(1)}, f32[1024,1024]{1,0:T(8,128)}, u32[]{:S(2)}) copy-start(f32[1024,1024]{1,0:T(8,128)} %get-tuple-element.37) | copy-start | bytes 12582916
  312.5 3.7 %copy-start.1 = (f32[1024,1024]{1,0:T(8,128)S(1)}, f32[1024,1024]{1,0:T(8,128)}, u32[]{:S(2)}) copy-start(f32[1024,1024]{1,0:T(8,128)} %get-tuple-element.38) | copy-start | bytes 12582916
  312.5 5.8 %slice-start = ((s8[8388608]{0:T(1024)(128)(4,1)}), s8[4194304]{0:T(1024)(128)(4,1)S(1)}, s32[]{:S(2)}) async-start(s8[8388608]{0:T(1024)(128)(4,1)} %bitcast.12), calls=%async_computation | async-start | bytes 8388608
  316.2 4.2 %slice-start.1 = ((s8[8388608]{0:T(1024)(128)(4,1)}), s8[4194304]{0:T(1024)(128)(4,1)S(1)}, s32[]{:S(2)}) async-start(s8[8388608]{0:T(1024)(128)(4,1)} %bitcast.12), calls=%async_computation.1 | async-start | bytes 8388608

commit v3 on v2

v3 whole, which is shorter than its diff:
```python
import math
import jax
import jax.numpy as jnp
import numpy as np
from jax import lax
from jax.experimental import pallas as pl
from jax.experimental.pallas import tpu as pltpu
from jax.sharding import PartitionSpec as P

ROPE_BASE = 1000000.0
NORM_EPS = 1e-6
LOG2E = 1.4426950408889634
F32 = jnp.float32
BF16 = jnp.bfloat16
QBLK = 256
VMEM_LIMIT = 35 * 1024 * 1024
COLOURS = ((1, 2, 3), (2, 3, 1), (3, 1, 2))
PER_POINT = 4
MASKS = (14, 12, 8, 6, 4, 10, 2, 15, 13, 9, 7, 5, 11, 3, 1)


def dot(a, b, ca, cb):
    return lax.dot_general(a, b, (((ca,), (cb,)), ((), ())), preferred_element_type=F32)


def rope_tables(n_pos, head_dim):
    half_dim = head_dim // 2
    inv_freq = np.exp(np.arange(half_dim, dtype=np.float32) * np.float32(-2.0 * math.log(ROPE_BASE) / head_dim))
    angles = np.arange(n_pos, dtype=np.float32)[:, None] * inv_freq[None, :]
    cos, sin = np.cos(angles), np.sin(angles)
    return np.concatenate([cos, cos], axis=-1), np.concatenate([-sin, sin], axis=-1)


def norm_rope(raw, gain, cos, sin):
    inv = lax.rsqrt(jnp.mean(raw * raw, axis=-1, keepdims=True) + NORM_EPS)
    unit = raw * inv
    normed = unit * gain
    return normed * cos + pltpu.roll(normed, raw.shape[-1] // 2, 1) * sin, unit, inv


def norm_rope_back(d_rot, unit, inv, gain, cos, sin):
    d_normed = d_rot * cos - pltpu.roll(d_rot, unit.shape[-1] // 2, 1) * sin
    d_gain = jnp.sum(d_normed * unit, axis=0, keepdims=True)
    d_unit = d_normed * gain
    return inv * (d_unit - unit * jnp.mean(d_unit * unit, axis=-1, keepdims=True)), d_gain


def causal_mask_t(scores_t, first_q):
    n_q = scores_t.shape[1]
    key = lax.broadcasted_iota(jnp.int32, (n_q, n_q), 0)
    query = lax.broadcasted_iota(jnp.int32, (n_q, n_q), 1)
    diag = jnp.where(query >= key, scores_t[first_q:], -1e30)
    if first_q == 0:
        return diag
    return jnp.concatenate([scores_t[:first_q], diag], axis=0)


def block_kernel(n_groups, *refs):
    n_steps = n_groups + 4

    def body(step, carry):
        block_step(step, n_steps, n_groups, *refs)
        return carry
    lax.fori_loop(0, n_steps, body, 0)


def block_step(step, n_steps, n_groups, hid_ref, dyin_ref, gain_ref, wq_ref, wk_ref, wv_ref, wo_ref, qg_ref, kg_ref,
               cos_ref, sin_ref, y_ref, dx_ref, u, small_ref,
               xs, dys, hs, ht, wcats, wos, dqkv, oall, y_acc, dn_acc, r0, r1, r2, r3, r4, sm, smr,
               in_send, in_recv, in_loc, d_send, d_recv, p_send, p_recv, g_send, g_recv, e_send, e_recv,
               s_send, s_recv, out_send, out_recv, out_loc, w_sem):
    n_dev, rows, n_loc, dim = hid_ref.shape
    n_pos = n_dev * n_loc
    head_dim = qg_ref.shape[-1]
    qw = wos.shape[1]
    group = qw // head_dim
    width = qw + 2 * head_dim
    half = u.shape[1] // 2
    lane = half // 2
    blk = lane // 3
    wcat, wo = wcats.at[step % 2], wos.at[step % 2]
    me = lax.axis_index('sp')
    bit = [(me // (1 << i)) % 2 for i in range(4)]
    partner = [me + (1 << i) * (1 - 2 * bit[i]) for i in range(4)]

    def remote(src, dst, send, recv, device):
        return pltpu.make_async_remote_copy(src_ref=src, dst_ref=dst, send_sem=send, recv_sem=recv,
                                            device_id=(device,), device_id_type=pl.DeviceIdType.MESH)

    def rows_of(g, start, size):
        return u.at[g, pl.ds(pl.multiple_of(start, 16), size)]

    own = [bit[0] * half + h * lane for h in range(2)]
    other = [(1 - bit[0]) * half + h * lane for h in range(2)]
    keep1, send1, keep2, send2, keep3, send3 = {}, {}, {}, {}, {}, {}
    for h in range(2):
        for c, (d1, d2, d3) in enumerate(COLOURS):
            base = own[h] + c * blk
            keep1[h, c] = base + bit[d1] * (blk // 2)
            send1[h, c] = base + (1 - bit[d1]) * (blk // 2)
            keep2[h, c] = keep1[h, c] + bit[d2] * (blk // 4)
            send2[h, c] = keep1[h, c] + (1 - bit[d2]) * (blk // 4)
            keep3[h, c] = keep2[h, c] + bit[d3] * (blk // 8)
            send3[h, c] = keep2[h, c] + (1 - bit[d3]) * (blk // 8)

    def core_scatter(g, h):
        return remote(rows_of(g, other[h], lane), r0.at[g % 2, h], d_send.at[h, g % 2], d_recv.at[h, g % 2], partner[0])

    def scatter(phase, c, g, h):
        start, size, buf = ((send1, blk // 2, r1), (send2, blk // 4, r2), (send3, blk // 8, r3))[phase]
        return remote(rows_of(g, start[h, c], size), buf.at[g % 2, h, c], p_send.at[phase, c, h, g % 2],
                      p_recv.at[phase, c, h, g % 2], partner[COLOURS[c][phase]])

    def gather(phase, c, g, h):
        start, size = ((keep3, blk // 8), (keep2, blk // 4), (keep1, blk // 2))[phase]
        part = rows_of(g, start[h, c], size)
        return remote(part, part if phase else r4.at[g % 2, h, c], g_send.at[phase, c, h, g % 2],
                      g_recv.at[phase, c, h, g % 2], partner[COLOURS[c][2 - phase]])

    def core_gather(g, h):
        part = rows_of(g, own[h], lane)
        return remote(part, part, e_send.at[h, g % 2], e_recv.at[h, g % 2], partner[0])

    def add_rows(g, start, size, buf):
        s = pl.ds(pl.multiple_of(start, 16), size)
        u[g, s] = u[g, s] + buf

    def stage(k, g, h):
        slot = g % 2
        if k == 1:
            core_scatter(g, h).wait()
            for c in range(3):
                add_rows(g, own[h] + c * blk, blk, r0[slot, h, c * blk:(c + 1) * blk])
                scatter(0, c, g, h).start()
        elif k in (2, 3, 4):
            keep, size, buf = ((keep1, blk // 2, r1), (keep2, blk // 4, r2), (keep3, blk // 8, r3))[k - 2]
            for c in range(3):
                scatter(k - 2, c, g, h).wait()
            for c in range(3):
                add_rows(g, keep[h, c], size, buf[slot, h, c])
                (scatter(k - 1, c, g, h) if k < 4 else gather(0, c, g, h)).start()
        elif k in (5, 6):
            for c in range(3):
                gather(k - 5, c, g, h).wait()
            for c in range(3):
                if k == 5:
                    u[g, pl.ds(pl.multiple_of(send3[h, c], 16), blk // 8)] = r4[slot, h, c]
                gather(k - 4, c, g, h).start()
        elif k == 7:
            for c in range(3):
                gather(2, c, g, h).wait()
            core_gather(g, h).start()
        else:
            core_gather(g, h).wait()

    sends = [(which, row, mask) for row in range(2) for which in (1, 0) for mask in MASKS]

    def handler(sub):
        h = sub % 2
        for k in range(8, 0, -1):
            if (2 * k - 2 + h - sub) % 4 == 0:
                g = step - 1 - (2 * k - 2 + h - sub) // 4

                @pl.when((g >= 0) & (g < n_groups))
                def _():
                    stage(k, g, h)
        for i in range(5):
            if (2 * i + 3) % 4 == sub:
                @pl.when(step == n_groups + (2 * i + 3) // 4)
                def _():
                    if i == 0:
                        small_copy(0).start()
                    else:
                        small_step(i - 1)
        for j in range(-(-len(sends) // PER_POINT)):
            if (j + 1) % 4 == sub:
                @pl.when(step == n_groups + (j + 1) // 4)
                def _():
                    for which, row, mask in sends[j * PER_POINT:(j + 1) * PER_POINT]:
                        to_peers(out_copy, which, row, (mask,))

    def small_copy(i):
        return remote(sm.at[i], smr.at[i], s_send.at[i], s_recv.at[i], partner[i])

    def small_step(i):
        small_copy(i).wait()
        sm[i + 1] = sm[i] + smr[i]
        if i < 3:
            small_copy(i + 1).start()
        else:
            small_ref[...] = sm[4]

    def in_copy(which, row, peer):
        src, dst = (hid_ref, xs) if which == 0 else (dyin_ref, dys)
        n = 2 * row + which
        return remote(src.at[peer, row], dst.at[row, me], in_send.at[n], in_recv.at[n], peer)

    def in_local(which, row):
        src, dst = (hid_ref, xs) if which == 0 else (dyin_ref, dys)
        return pltpu.make_async_copy(src.at[me, row], dst.at[row, me], in_loc.at[2 * row + which])

    def in_wait(which, row):
        dst = xs if which == 0 else dys
        n = 2 * row + which
        many = dst.at[row, pl.ds(0, n_dev - 1)]
        pltpu.make_async_copy(many, many, in_recv.at[n]).wait()
        in_local(which, row).wait()

    def in_wait_send(which, row):
        many = (xs if which == 0 else dys).at[row, pl.ds(0, n_dev - 1)]
        pltpu.make_async_copy(many, many, in_send.at[2 * row + which]).wait()

    def out_copy(which, row, peer):
        src, dst = (xs, y_ref) if which == 0 else (dys, dx_ref)
        n = 2 * row + which
        return remote(src.at[row, peer], dst.at[me, row], out_send.at[n], out_recv.at[n], peer)

    def out_local(which, row):
        src, dst = (xs, y_ref) if which == 0 else (dys, dx_ref)
        return pltpu.make_async_copy(src.at[row, me], dst.at[me, row], out_loc.at[2 * row + which])

    def to_peers(make, which, row, masks):
        for mask in masks:
            make(which, row, me + sum((mask & (1 << i)) * (1 - 2 * bit[i]) for i in range(4))).start()

    @pl.when(step == 0)
    def _():
        barrier = pltpu.get_barrier_semaphore()

        def greet(d, carry):
            pl.semaphore_signal(barrier, inc=1, device_id=(lax.rem(me + d, n_dev),), device_id_type=pl.DeviceIdType.MESH)
            return carry
        lax.fori_loop(1, n_dev, greet, 0)
        pl.semaphore_wait(barrier, n_dev - 1)
        for row in range(rows):
            for which in range(2):
                in_local(which, row).start()
                to_peers(in_copy, which, row, MASKS)
        y_acc[...] = jnp.zeros_like(y_acc)
        dn_acc[...] = jnp.zeros_like(dn_acc)
        sm[0] = jnp.zeros_like(sm[0])

    def tokens_of(row):
        return slice(row * n_pos, (row + 1) * n_pos)

    def row_compute(row):
        tok = tokens_of(row)
        cos, sin = cos_ref[...], sin_ref[...]
        scale = head_dim ** -0.5
        qkv = dot(hs[tok], wcat[...], 1, 0).astype(BF16)

        @pl.when(step == 0)
        def _():
            in_wait(1, row)
        d_o = dot(dys[row].reshape(n_pos, dim), wo[...], 1, 1).astype(BF16)
        k_rot, k_unit, k_inv = norm_rope(qkv[:, qw:qw + head_dim].astype(F32), kg_ref[...], cos, sin)
        k_rot = k_rot.astype(BF16)
        v = qkv[:, qw + head_dim:]
        dk_sum = [jnp.zeros((QBLK, head_dim), F32) for _ in range(n_pos // QBLK)]
        dv_sum = [jnp.zeros((QBLK, head_dim), F32) for _ in range(n_pos // QBLK)]
        for j in range(group):
            cols = slice(j * head_dim, (j + 1) * head_dim)
            q_rot, q_unit, q_inv = norm_rope(qkv[:, cols].astype(F32), qg_ref[...], cos, sin)
            q_rot = q_rot.astype(BF16)
            dq_parts = []
            for first in range(0, n_pos, QBLK):
                n_key = first + QBLK
                q_blk = q_rot[first:n_key]
                do_blk = d_o[first:n_key, cols]
                scores = causal_mask_t(dot(k_rot[:n_key], q_blk, 1, 1) * (scale * LOG2E), first)
                e = jnp.exp2(scores - jnp.max(scores, axis=0, keepdims=True))
                prob = e * (1.0 / jnp.sum(e, axis=0, keepdims=True))
                prob_bf = prob.astype(BF16)
                oall[row * n_pos + first:row * n_pos + n_key, cols] = dot(prob_bf, v[:n_key], 0, 0).astype(BF16)
                d_prob = dot(v[:n_key], do_blk, 1, 1)
                inner = jnp.sum(prob * d_prob, axis=0, keepdims=True)
                d_scores = (prob * (d_prob - inner) * scale).astype(BF16)
                dv_blk = dot(prob_bf, do_blk, 1, 0)
                dk_blk = dot(d_scores, q_blk, 1, 0)
                for i in range(n_key // QBLK):
                    dv_sum[i] += dv_blk[i * QBLK:(i + 1) * QBLK]
                    dk_sum[i] += dk_blk[i * QBLK:(i + 1) * QBLK]
                dq_parts.append(dot(d_scores, k_rot[:n_key], 0, 0))
            dq = jnp.concatenate(dq_parts, axis=0).astype(BF16).astype(F32)
            dq_raw, d_gain = norm_rope_back(dq, q_unit, q_inv, qg_ref[...], cos, sin)
            dqkv[tok, cols] = dq_raw.astype(BF16)
            sm[0, 1:2, :head_dim] += d_gain
        dk = jnp.concatenate(dk_sum, axis=0).astype(BF16).astype(F32)
        dk_raw, d_gain = norm_rope_back(dk, k_unit, k_inv, kg_ref[...], cos, sin)
        dqkv[tok, qw:qw + head_dim] = dk_raw.astype(BF16)
        sm[0, 1:2, head_dim:2 * head_dim] += d_gain
        dqkv[tok, qw + head_dim:] = jnp.concatenate(dv_sum, axis=0).astype(BF16)

    def input_norm(row):
        x = xs[row].reshape(n_pos, dim).astype(F32)
        inv = lax.rsqrt(jnp.mean(x * x, axis=-1, keepdims=True) + NORM_EPS)
        h = (x * inv * gain_ref[...]).astype(BF16)
        hs[tokens_of(row)] = h
        ht[:, tokens_of(row)] = h.T

    def finish_row(row):
        tok = tokens_of(row)
        x = xs[row].reshape(n_pos, dim).astype(F32)
        inv = lax.rsqrt(jnp.mean(x * x, axis=-1, keepdims=True) + NORM_EPS)
        unit = x * inv
        d_normed = dn_acc[tok]
        sm[0, 0:1] += jnp.sum(d_normed * unit, axis=0, keepdims=True)
        d_unit = d_normed * gain_ref[...]
        d_x = inv * (d_unit - unit * jnp.mean(d_unit * unit, axis=-1, keepdims=True))
        d_y = dys[row].reshape(n_pos, dim).astype(F32)
        dys[row] = (d_y + d_x).astype(BF16).reshape(n_dev, n_loc, dim)
        xs[row] = (x + y_acc[tok]).astype(BF16).reshape(n_dev, n_loc, dim)

    computing = step < n_groups

    def weight_copies(g):
        slot = g % 2
        col = lambda n: pl.ds(pl.multiple_of(g * n, 128), n)
        pieces = ((wq_ref.at[:, col(qw)], wcats.at[slot, :, :qw]),
                  (wk_ref.at[:, col(head_dim)], wcats.at[slot, :, qw:qw + head_dim]),
                  (wv_ref.at[:, col(head_dim)], wcats.at[slot, :, qw + head_dim:]),
                  (wo_ref.at[col(qw)], wos.at[slot]))
        return [pltpu.make_async_copy(a, b, w_sem.at[slot, i]) for i, (a, b) in enumerate(pieces)]

    @pl.when(computing)
    def _():
        @pl.when(step == 0)
        def _():
            for copy in weight_copies(0):
                copy.start()
        for copy in weight_copies(step):
            copy.wait()

        @pl.when(step + 1 < n_groups)
        def _():
            for copy in weight_copies(step + 1):
                copy.start()

    for row in range(rows):
        handler(row)

        @pl.when(step == 0)
        def _():
            in_wait(0, row)
            input_norm(row)

        @pl.when(computing)
        def _():
            row_compute(row)

        @pl.when(step == n_groups)
        def _():
            for which in range(2):
                in_wait_send(which, row)
            finish_row(row)
            for which in range(2):
                out_local(which, row).start()

    handler(2)

    @pl.when(computing)
    def _():
        u[step, :dim] = dot(ht[...], dqkv[...], 1, 0)
        d_wo = dot(oall[...], dys[...].reshape(rows * n_pos, dim), 0, 0)
        u[step, dim:dim + qw] = d_wo[:, :width]
        u[step, dim + qw:] = d_wo[:, width:]
        for h in range(2):
            core_scatter(step, h).start()

    handler(3)

    @pl.when(computing)
    def _():
        y_acc[...] += dot(oall[...], wo[...], 1, 0)
        dn_acc[...] += dot(dqkv[...], wcat[...], 1, 1)

    @pl.when(step == n_steps - 1)
    def _():
        for row in range(rows):
            for which in range(2):
                n = 2 * row + which
                many = (xs if which == 0 else dys).at[row, pl.ds(0, n_dev - 1)]
                landed = (y_ref if which == 0 else dx_ref).at[pl.ds(0, n_dev - 1), row]
                pltpu.make_async_copy(many, many, out_send.at[n]).wait()
                pltpu.make_async_copy(landed, landed, out_recv.at[n]).wait()
                out_local(which, row).wait()


def place_kernel(y_in, dx_in, u, small, y_ref, dx_ref, dwq_ref, dwk_ref, dwv_ref, dwo_ref, dg_ref, dqg_ref, dkg_ref,
                 out_sem, w_sem, s_sem):
    dim, head_dim = dg_ref.shape[1], dqg_ref.shape[1]
    n_groups, _, width = u.shape
    qw = dwq_ref.shape[1] // n_groups
    stores = []
    for g in range(n_groups):
        col = lambda n: slice(g * n, (g + 1) * n)
        pieces = ((u.at[g, :dim, :qw], dwq_ref.at[:, col(qw)]),
                  (u.at[g, :dim, qw:qw + head_dim], dwk_ref.at[:, col(head_dim)]),
                  (u.at[g, :dim, qw + head_dim:], dwv_ref.at[:, col(head_dim)]),
                  (u.at[g, dim:dim + qw], dwo_ref.at[col(qw), :width]),
                  (u.at[g, dim + qw:], dwo_ref.at[col(qw), width:]))
        stores += [pltpu.make_async_copy(src, dst, w_sem.at[g, i]) for i, (src, dst) in enumerate(pieces)]
    stores += [pltpu.make_async_copy(src, dst, s_sem.at[i]) for i, (src, dst) in enumerate((
        (small.at[0:1], dg_ref), (small.at[1:2, :head_dim], dqg_ref), (small.at[1:2, head_dim:2 * head_dim], dkg_ref)))]
    stores += [pltpu.make_async_copy(src, dst, out_sem.at[i]) for i, (src, dst) in enumerate(((y_in, y_ref), (dx_in, dx_ref)))]
    for copy in stores:
        copy.start()
    for copy in stores:
        copy.wait()


def solution(mesh):
    n_dev = mesh.shape['sp']
    seq_spec = P(None, 'sp', None)
    replicated = P()

    def local_step(hidden, norm_gain, w_q, w_k, w_v, q_gain, k_gain, w_o, d_out):
        n_batch, n_loc, dim = hidden.shape
        head_dim = q_gain.shape[0]
        kv_heads = w_k.shape[1] // head_dim
        qw = w_q.shape[1] // kv_heads
        width = qw + 2 * head_dim
        rows = n_batch // n_dev
        n_pos = n_loc * n_dev
        tokens = rows * n_pos
        cos, sin = rope_tables(n_pos, head_dim)
        slice_rows = dim + 2 * qw
        lane = slice_rows // 4
        blk = lane // 3
        anywhere = pl.BlockSpec(memory_space=pl.ANY)
        in_vmem = pl.BlockSpec(memory_space=pltpu.VMEM)
        act = (n_dev, rows, n_loc, dim)
        dma = pltpu.SemaphoreType.DMA
        y, d_hidden, slices, small = pl.pallas_call(
            lambda *refs: block_kernel(kv_heads, *refs),
            in_specs=[anywhere, anywhere, in_vmem, anywhere, anywhere, anywhere, anywhere] + [in_vmem] * 4,
            out_specs=[in_vmem] * 4,
            out_shape=[
                pltpu.VMEM(act, BF16), pltpu.VMEM(act, BF16),
                pltpu.VMEM((kv_heads, slice_rows, width), F32), pltpu.VMEM((8, dim), F32)],
            scratch_shapes=[
                pltpu.VMEM((rows, n_dev, n_loc, dim), BF16), pltpu.VMEM((rows, n_dev, n_loc, dim), BF16),
                pltpu.VMEM((tokens, dim), BF16), pltpu.VMEM((dim, tokens), BF16),
                pltpu.VMEM((2, dim, width), BF16), pltpu.VMEM((2, qw, dim), BF16),
                pltpu.VMEM((tokens, width), BF16), pltpu.VMEM((tokens, qw), BF16),
                pltpu.VMEM((tokens, dim), F32), pltpu.VMEM((tokens, dim), F32),
                pltpu.VMEM((2, 2, lane, width), F32), pltpu.VMEM((2, 2, 3, blk // 2, width), F32),
                pltpu.VMEM((2, 2, 3, blk // 4, width), F32), pltpu.VMEM((2, 2, 3, blk // 8, width), F32),
                pltpu.VMEM((2, 2, 3, blk // 8, width), F32),
                pltpu.VMEM((5, 8, dim), F32), pltpu.VMEM((4, 8, dim), F32),
                dma((4,)), dma((4,)), dma((4,)), dma((2, 2)), dma((2, 2)), dma((3, 3, 2, 2)), dma((3, 3, 2, 2)),
                dma((3, 3, 2, 2)), dma((3, 3, 2, 2)), dma((2, 2)), dma((2, 2)), dma((4,)), dma((4,)),
                dma((4,)), dma((4,)), dma((4,)), dma((2, 4))],
            compiler_params=pltpu.CompilerParams(
                vmem_limit_bytes=VMEM_LIMIT, collective_id=0, has_side_effects=True),
            cost_estimate=pl.CostEstimate(flops=52 * 10**9, bytes_accessed=50 * 10**6, transcendentals=0),
            name='attn_block',
        )(hidden.reshape(act), d_out.reshape(act), norm_gain[None], w_q, w_k, w_v, w_o, q_gain[None], k_gain[None],
          jnp.asarray(cos), jnp.asarray(sin))
        y, d_hidden, d_wq, d_wk, d_wv, d_wo, d_ng, d_qg, d_kg = pl.pallas_call(
            place_kernel,
            in_specs=[in_vmem] * 4,
            out_specs=[anywhere] * 9,
            out_shape=[
                jax.ShapeDtypeStruct(act, BF16), jax.ShapeDtypeStruct(act, BF16),
                jax.ShapeDtypeStruct(w_q.shape, F32), jax.ShapeDtypeStruct(w_k.shape, F32),
                jax.ShapeDtypeStruct(w_v.shape, F32), jax.ShapeDtypeStruct(w_o.shape, F32),
                jax.ShapeDtypeStruct((1, dim), F32), jax.ShapeDtypeStruct((1, head_dim), F32),
                jax.ShapeDtypeStruct((1, head_dim), F32)],
            scratch_shapes=[dma((2,)), dma((kv_heads, 5)), dma((3,))],
            compiler_params=pltpu.CompilerParams(vmem_limit_bytes=4 * 1024 * 1024),
            cost_estimate=pl.CostEstimate(flops=10**9, bytes_accessed=60 * 10**6, transcendentals=0),
            name='pack_out',
        )(*[pltpu.with_memory_space_constraint(a, pltpu.VMEM) for a in (y, d_hidden, slices, small)])
        return (y.reshape(hidden.shape), d_hidden.reshape(hidden.shape), d_wq, d_wk, d_wv, d_wo, d_ng[0], d_qg[0], d_kg[0])

    return jax.shard_map(local_step, mesh=mesh, in_specs=(seq_spec, replicated, replicated, replicated, replicated, replicated, replicated, replicated, seq_spec), out_specs=(seq_spec, seq_spec, replicated, replicated, replicated, replicated, replicated, replicated, replicated), check_vma=False)
```

time: 324 us -> 286 us (0.88)
  local copies, waits for them, and re-layouts: 26 us -> 0 us
  Pallas kernels: 297 us -> 285 us
    unnamed x16 -> x0, local copies, waits for them, and re-layouts: 23.5 us -> none
    pallas_call x1 -> x2, Pallas kernels: 297 us -> 285 us  [the longest x1 275 us: local_step(): pl.pallas_call(lambda *refs: block_kernel(kv_heads, *refs), in_specs=[any...]
where the time goes in v3:
time: 286 us
  Pallas kernels  285 us (100%)
    pallas_call x1, Pallas kernels, local_step(): pl.pallas_call(lambda *refs: block_kernel(kv_heads, *refs), in_specs=[any...  275 us
    pallas_call x1, Pallas kernels, local_step(): pl.pallas_call(place_kernel, in_specs=[in_vmem] * 4, out_specs=[anywhere]...  10 us

profile of v3, /device:TPU:0, one launch (start us, length us, event | category | flops | bytes accessed | tf_op | source)
XLA Modules:
  0.0 285.8 jit_solution(9667174804581083517)
XLA Ops:
  0.6 275.1 %attn_block.1 = (bf16[16,2,32,1024]{3,2,1,0:T(8,128)(2,1)S(1)}, bf16[16,2,32,1024]{3,2,1,0:T(8,128)(2,1)S(1)}, f32[8,1536,512]{2,1,0:T(8,128)S(1)}, f32[8,1024]{1,0:T(8,128)S(1)}) custom-call(bf16[16,2,32,1024]{3,2,1,0:T(8,128)(2,1)} %bitcast.10, bf16[16,2,32,1024]{3,2,1,0:T(8,128)(2,1)} %bitcast.11, f32[1,1024]{1,0:T(1,128)} %bitcast.14, ...), custom_call_target="tpu_custom_call" | custom-call | flops 51999997952 | bytes 50000000 | tf_op jit(solution)/shard_map/attn_block/pallas_call | solution.py:434
  275.7 10.0 %pack_out.1 = (bf16[16,2,32,1024]{3,2,1,0:T(8,128)(2,1)}, bf16[16,2,32,1024]{3,2,1,0:T(8,128)(2,1)}, f32[1024,2048]{1,0:T(8,128)}, f32[1024,1024]{1,0:T(8,128)},...) custom-call(bf16[16,2,32,1024]{3,2,1,0:T(8,128)(2,1)S(1)} %get-tuple, ...), custom_call_target="tpu_custom_call" | custom-call | flops 1000000000 | bytes 60000000 | tf_op jit(solution)/shard_map/pack_out/pallas_call | solution.py:460
